TPU v7x, 16 devices: a 4x2x1 block of a 4x4x8 slice. The times are simulated.
16 devices in a mesh: dp: 2 (over y, z), tp: 8 (over x, core).
Axes of the slice: x: 4, y: 2, z: 1, core: 2. Of those that a mesh axis runs over, the one named last changes fastest.
The devices are a block of a 4x4x8 slice.
Arguments:
- hidden: bfloat16 [256, 5120], P('dp'), parts along dimension 0
- lengths: int32 [256], P('dp'), parts along dimension 0
- k_cache: bfloat16 [2, 256, 128, 8, 128], P(None, 'dp', None, 'tp'), parts along dimension 1
- v_cache: bfloat16 [2, 256, 128, 8, 128], P(None, 'dp', None, 'tp'), parts along dimension 1
- attn_norm: bfloat16 [2, 5120], replicated
- w_qkv: bfloat16 [2, 5120, 8, 768], P(None, None, 'tp')
- w_out: bfloat16 [2, 4096, 5120], P(None, 'tp')
- mlp_norm: bfloat16 [2, 5120], replicated
- w_gate: bfloat16 [2, 5120, 14336], P(None, None, 'tp')
- w_up: bfloat16 [2, 5120, 14336], P(None, None, 'tp')
- w_down: bfloat16 [2, 14336, 5120], P(None, 'tp')
Outputs:
- output: bfloat16 [256, 5120], P('dp'), parts along dimension 0
There are 2 independent parts. A program takes and returns all parts, laid end to end along the dimension named above; an argument that names none is the same for every part.
All inputs are finite; a program needn't handle non-finite values.
Results may differ from a plain program's by a relative error of at most 0.0187289.
Values are sent between devices in bfloat16 or wider.
A program may use at most 768 MiB of HBM per device.

v0:
```python
import jax
import jax.numpy as jnp
from jax import lax
from jax.sharding import PartitionSpec as P

ROPE_BASE = 10000.0
NORM_EPS = 1e-5


def rms_norm(values, gain):
    wide = values.astype(jnp.float32)
    scale = lax.rsqrt(jnp.mean(wide * wide, axis=-1, keepdims=True) + NORM_EPS)
    return (wide * scale * gain.astype(jnp.float32)).astype(jnp.bfloat16)


def rotate(values, cosine, sine):
    half = values.shape[-1] // 2
    first = values[..., :half]
    second = values[..., half:]
    return jnp.concatenate([first * cosine - second * sine, second * cosine + first * sine], axis=-1)


def rope_tables(lengths, head_dim):
    inv_freq = ROPE_BASE ** (-jnp.arange(0, head_dim, 2, dtype=jnp.float32) / head_dim)
    angles = lengths.astype(jnp.float32)[:, None] * inv_freq[None, :]
    return jnp.cos(angles), jnp.sin(angles)


def attention(fused, keys_layer, values_layer, live, cosine, sine):
    group = fused.shape[2] - 2
    scale = fused.shape[3] ** -0.5
    wide = fused.astype(jnp.float32)
    query = rotate(wide[:, :, :group], cosine[:, None, None, :], sine[:, None, None, :]).astype(jnp.bfloat16)
    key_new = rotate(wide[:, :, group], cosine[:, None, :], sine[:, None, :]).astype(jnp.bfloat16)
    val_new = fused[:, :, group + 1]
    logits = jnp.einsum('bkgd,bskd->bkgs', query, keys_layer, preferred_element_type=jnp.float32) * scale
    logits = jnp.where(live[:, None, None, :], logits, -1e30)
    self_logit = jnp.einsum('clhe,cle->clh', query, key_new, preferred_element_type=jnp.float32) * scale
    peak = jnp.maximum(jnp.max(logits, axis=-1), self_logit)
    weights = jnp.exp(logits - peak[..., None]).astype(jnp.bfloat16)
    self_weight = jnp.exp(self_logit - peak).astype(jnp.bfloat16).astype(jnp.float32)
    denominator = jnp.sum(weights, axis=-1, dtype=jnp.float32) + self_weight
    numerator = jnp.einsum('bkgs,bskd->bkgd', weights, values_layer, preferred_element_type=jnp.float32)
    numerator = numerator + self_weight[..., None] * val_new.astype(jnp.float32)[:, :, None, :]
    return (numerator / denominator[..., None]).astype(jnp.bfloat16)


def solution(mesh):
    group_devs = mesh.shape['tp']

    def reduce_add(partial, residual):
        rows, d_model = partial.shape
        width = d_model // group_devs
        pieces = lax.all_to_all(partial.reshape(rows, group_devs, width), 'tp', 1, 1, tiled=True)
        own_part = lax.dynamic_slice_in_dim(residual, lax.axis_index('tp') * width, width, axis=1)
        summed = (own_part.astype(jnp.float32) + jnp.sum(pieces, axis=1, dtype=jnp.float32)).astype(jnp.bfloat16)
        return lax.all_gather(summed, 'tp', axis=1, tiled=True)

    def local_step(hidden, lengths, k_cache, v_cache, attn_norm, w_qkv, w_out, mlp_norm, w_gate, w_up, w_down):
        rows = hidden.shape[0]
        head_dim = k_cache.shape[4]
        cosine, sine = rope_tables(lengths, head_dim)
        live = jnp.arange(k_cache.shape[2])[None, :] < lengths[:, None]
        residual = hidden
        for layer in range(w_qkv.shape[0]):
            normed = rms_norm(residual, attn_norm[layer])
            fused = jnp.einsum('bd,dkf->bkf', normed, w_qkv[layer], preferred_element_type=jnp.float32).astype(jnp.bfloat16)
            fused = fused.reshape(rows, fused.shape[1], -1, head_dim)
            attended = attention(fused, k_cache[layer], v_cache[layer], live, cosine, sine)
            partial = jnp.dot(attended.reshape(rows, -1), w_out[layer], preferred_element_type=jnp.float32).astype(jnp.bfloat16)
            residual = reduce_add(partial, residual)
            normed = rms_norm(residual, mlp_norm[layer])
            gate_proj = jnp.dot(normed, w_gate[layer], preferred_element_type=jnp.float32).astype(jnp.bfloat16)
            up_proj = jnp.dot(normed, w_up[layer], preferred_element_type=jnp.float32).astype(jnp.bfloat16)
            activated = (jax.nn.silu(gate_proj.astype(jnp.float32)) * up_proj.astype(jnp.float32)).astype(jnp.bfloat16)
            partial = jnp.dot(activated, w_down[layer], preferred_element_type=jnp.float32).astype(jnp.bfloat16)
            residual = reduce_add(partial, residual)
        return residual

    cache_spec = P(None, 'dp', None, 'tp', None)
    in_specs = (P('dp', None), P('dp'), cache_spec, cache_spec, P(), P(None, None, 'tp', None),
                P(None, 'tp', None), P(), P(None, None, 'tp'), P(None, None, 'tp'), P(None, 'tp', None))
    return jax.shard_map(local_step, mesh=mesh, in_specs=in_specs, out_specs=P('dp', None), check_vma=False)
```

profile of v0, /device:TPU:113, one launch (start us, length us, event | category | flops | bytes accessed | tf_op | source)
XLA Modules:
  0.0 285.0 jit_solution(125919770243233319)
XLA Ops:
  6.6 0.7 convert_element_type.214
  7.2 0.7 iota_compare_fusion
  8.0 1.7 fusion.38
  9.6 0.8 slice_convert_fusion.1
  10.5 4.9 %fusion.92 = bf16[128,768]{1,0:T(8,128)(2,1)S(1)} fusion(bf16[2,5120,1,768]{3,1,2,0:T(8,128)(2,1)} %param.16, bf16[128,5120]{1,0:T(8,128)(2,1)} %param.11, f32[5120]{0:T(1024)S(1)} %bitcast.198, f32[128]{0:T(128)S(1)} %add_rsqrt_fusion.3), kind=kOutput, calls=%fused_computation.84 | convolution fusion | flops 1009352704 | bytes 9392640 | tf_op jit(solution)/shard_map/bd,dkf->bkf/dot_general | solution.py:67
  15.4 0.2 copy.59
  15.6 0.1 copy.63
  15.7 0.2 multiply_cosine_fusion.1
  15.9 0.2 fusion.147
  16.2 0.1 copy.61
  16.3 0.1 copy.73
  16.5 0.3 fusion.154
  16.7 4.5 %fusion.152 = (f32[128,4]{1,0:T(8,128)S(1)}, f32[128,4,128]{2,1,0:T(4,128)S(1)}) fusion(bf16[128,4,128]{2,1,0:T(4,128)(2,1)S(1)} %copy.61, bf16[2,128,128,1,128]{4,2,1,3,0:T(8,128)(2,1)} %bitcast.199, pred[128,128]{1,0:T(8,128)(4,1)S(1)} %iota_compare_fusion), kind=kOutput, calls=%fused_computation.168 | convolution fusion | flops 16973312 | bytes 4605952 | tf_op jit(solution)/shard_map/bkgd,bskd->bkgs/dot_general | solution.py:36
  21.3 0.4 convert_reduce_fusion.5
  21.7 3.5 %fusion.111 = bf16[128,4,128]{2,1,0:T(4,128)(2,1)S(1)} fusion(bf16[2,128,128,1,128]{4,2,1,3,0:T(8,128)(2,1)} %bitcast.201, f32[128,4]{1,0:T(8,128)S(1)} %get-tuple-element.7, f32[128,128]{1,0:T(8,128)S(1)} %copy.63, f32[128,4]{1,0:T(8,128)S(1)} %get-tuple-element.8, f32[128,4,128]{2,1,0:T(4,128)S(1)} %get-tuple-element.24, ...), kind=kOutput, calls=%fused_computation.95 | convolution fusion | flops 17170432 | bytes 4659200 | tf_op jit(solution)/shard_map/bkgs,bskd->bkgd/dot_general | solution.py:43
  25.2 3.3 %convolution_convert_fusion.1 = bf16[128,5120]{1,0:T(8,128)(2,1)S(1)} fusion(bf16[2,512,5120]{2,1,0:T(8,128)(2,1)} %param.17, bf16[16,8,4,128]{3,2,1,0:T(4,128)(2,1)S(1)} %bitcast.203), kind=kOutput, calls=%fused_computation.27 | convolution fusion | flops 671744000 | bytes 6684672 | tf_op jit(solution)/shard_map/dot_general | solution.py:70
  28.6 1.2 copy.98
  29.7 6.1 %all-to-all-start = ((bf16[128,8,640]{2,0,1:T(8,128)(2,1)}), bf16[128,8,640]{2,0,1:T(8,128)(2,1)S(1)}, u32[]{:S(2)}, u32[]{:S(2)}) async-start(bf16[128,8,640]{2,0,1:T(8,128)(2,1)} %bitcast.177), calls=%async_computation | async-start | bytes 2621440 | tf_op jit(solution)/shard_map/all_to_all | solution.py:54
  35.9 17.6 %all-to-all-done = bf16[128,8,640]{2,0,1:T(8,128)(2,1)S(1)} async-done(((bf16[128,8,640]{2,0,1:T(8,128)(2,1)}), bf16[128,8,640]{2,0,1:T(8,128)(2,1)S(1)}, u32[]{:S(2)}, u32[]{:S(2)}) %all-to-all-start) | async-done | bytes 1310752 | tf_op jit(solution)/shard_map/all_to_all | solution.py:54
  53.5 0.2 convert_reduce_fusion.3
  53.6 1.6 add_convert_fusion.3
  55.3 0.1 all-gather.5.cloned.1.call-update
  55.3 0.2 all-gather.7.cloned.1.call-start
  55.6 20.4 %all-gather.5.cloned.1.call-done = bf16[128,5120]{1,0:T(8,128)(2,1)} async-done(((bf16[128,640]{1,0:T(8,128)(2,1)}), bf16[128,5120]{1,0:T(8,128)(2,1)}) %all-gather.5.cloned.1.call-update) | async-done | bytes 1310736 | tf_op jit(solution)/shard_map/all_gather | solution.py:57
  76.0 1.6 fusion.41
  77.6 8.3 %fusion.53 = f32[128,1792]{1,0:T(8,128)S(1)} fusion(bf16[2,5120,1792]{2,1,0:T(8,128)(2,1)} %param.19, bf16[128,5120]{1,0:T(8,128)(2,1)} %all-gather.5.cloned.1.call-done, f32[5120]{0:T(1024)S(1)} %bitcast.196, f32[128]{0:T(128)S(1)} %add_rsqrt_fusion.2), kind=kOutput, calls=%fused_computation.65 | convolution fusion | flops 2351890432 | bytes 20599296 | tf_op jit(solution)/shard_map/dot_general | solution.py:73
  86.0 7.9 %fusion.65 = bf16[128,1792]{1,0:T(8,128)(2,1)S(1)} fusion(bf16[2,5120,1792]{2,1,0:T(8,128)(2,1)} %param.20, f32[128,1792]{1,0:T(8,128)S(1)} %fusion.53, bf16[128,5120]{1,0:T(8,128)(2,1)S(1)} %copy-done, f32[5120]{0:T(1024)S(1)} %bitcast.197, f32[128]{0:T(128)S(1)} %add_rsqrt_fusion.2), kind=kOutput, calls=%fused_computation.69 | convolution fusion | flops 2353266688 | bytes 21058048 | tf_op jit(solution)/shard_map/dot_general | solution.py:74
  93.9 8.9 %fusion.24 = bf16[128,5120]{1,0:T(8,128)(2,1)S(1)} fusion(bf16[128,1792]{1,0:T(8,128)(2,1)S(1)} %fusion.65, bf16[2,1792,5120]{2,1,0:T(8,128)(2,1)} %param.21), kind=kOutput, calls=%fused_computation.24 | convolution fusion | flops 2349465600 | bytes 20119552 | tf_op jit(solution)/shard_map/dot_general | solution.py:76
  102.8 0.1 copy.97
  103.0 20.9 %all_to_all.20 = bf16[128,8,640]{2,0,1:T(8,128)(2,1)S(1)} all-to-all(bf16[128,8,640]{2,0,1:T(8,128)(2,1)S(1)} %bitcast.178), channel_id=1, replica_groups=mesh['dp'=2,'tp'=8] {'tp'}, dimensions={1} | all-to-all | bytes 2621440 | tf_op jit(solution)/shard_map/all_to_all | solution.py:54
  123.8 0.2 convert_reduce_fusion.2
  124.0 0.7 add_convert_fusion.2
  124.7 0.1 all-gather.7.cloned.1.call-update
  124.8 0.3 all-gather.9.cloned.1.call-start
  125.1 19.7 %all-gather.7.cloned.1.call-done = bf16[128,5120]{1,0:T(8,128)(2,1)} async-done(((bf16[128,640]{1,0:T(8,128)(2,1)}), bf16[128,5120]{1,0:T(8,128)(2,1)}) %all-gather.7.cloned.1.call-update) | async-done | bytes 1310736 | tf_op jit(solution)/shard_map/all_gather | solution.py:57
  144.8 1.6 fusion.44
  146.4 4.9 %fusion.97 = bf16[128,768]{1,0:T(8,128)(2,1)S(1)} fusion(bf16[2,5120,1,768]{3,1,2,0:T(8,128)(2,1)} %param.16, bf16[128,5120]{1,0:T(8,128)(2,1)} %all-gather.7.cloned.1.call-done, f32[5120]{0:T(1024)S(1)} %bitcast.193, f32[128]{0:T(128)S(1)} %add_rsqrt_fusion.1), kind=kOutput, calls=%fused_computation.85 | convolution fusion | flops 1009352704 | bytes 9392640 | tf_op jit(solution)/shard_map/bd,dkf->bkf/dot_general | solution.py:67
  151.4 0.2 copy.66
  151.6 0.1 copy.70
  151.7 0.2 fusion.145
  152.0 0.1 copy.68
  152.1 0.1 copy.75
  152.3 4.5 %fusion.153 = (f32[128,4]{1,0:T(8,128)S(1)}, f32[128,4,128]{2,1,0:T(4,128)S(1)}) fusion(bf16[128,4,128]{2,1,0:T(4,128)(2,1)S(1)} %copy.68, bf16[2,128,128,1,128]{4,2,1,3,0:T(8,128)(2,1)} %bitcast.200, pred[128,128]{1,0:T(8,128)(4,1)S(1)} %iota_compare_fusion), kind=kOutput, calls=%fused_computation.169 | convolution fusion | flops 16973312 | bytes 4605952 | tf_op jit(solution)/shard_map/bkgd,bskd->bkgs/dot_general | solution.py:36
  156.8 0.3 fusion.155
  157.1 0.4 convert_reduce_fusion.4
  157.5 3.5 %fusion.109 = bf16[128,4,128]{2,1,0:T(4,128)(2,1)S(1)} fusion(bf16[2,128,128,1,128]{4,2,1,3,0:T(8,128)(2,1)} %bitcast.202, f32[128,4]{1,0:T(8,128)S(1)} %get-tuple-element.5, f32[128,128]{1,0:T(8,128)S(1)} %copy.70, f32[128,4]{1,0:T(8,128)S(1)} %get-tuple-element.6, f32[128,4,128]{2,1,0:T(4,128)S(1)} %get-tuple-element.26, ...), kind=kOutput, calls=%fused_computation.93 | convolution fusion | flops 17170432 | bytes 4659200 | tf_op jit(solution)/shard_map/bkgs,bskd->bkgd/dot_general | solution.py:43
  161.0 3.4 %convolution_convert_fusion = bf16[128,5120]{1,0:T(8,128)(2,1)S(1)} fusion(bf16[2,512,5120]{2,1,0:T(8,128)(2,1)} %param.17, bf16[16,8,4,128]{3,2,1,0:T(4,128)(2,1)S(1)} %bitcast.204), kind=kOutput, calls=%fused_computation.26 | convolution fusion | flops 671744000 | bytes 6684672 | tf_op jit(solution)/shard_map/dot_general | solution.py:70
  164.4 0.1 copy.96
  164.5 20.9 %all_to_all.21 = bf16[128,8,640]{2,0,1:T(8,128)(2,1)S(1)} all-to-all(bf16[128,8,640]{2,0,1:T(8,128)(2,1)S(1)} %bitcast.179), channel_id=1, replica_groups=mesh['dp'=2,'tp'=8] {'tp'}, dimensions={1} | all-to-all | bytes 2621440 | tf_op jit(solution)/shard_map/all_to_all | solution.py:54
  185.4 0.2 convert_reduce_fusion.1
  185.5 1.6 add_convert_fusion.1
  187.1 0.1 all-gather.9.cloned.1.call-update
  187.2 0.3 all-gather.11.cloned.1.call-start
  187.5 19.7 %all-gather.9.cloned.1.call-done = bf16[128,5120]{1,0:T(8,128)(2,1)} async-done(((bf16[128,640]{1,0:T(8,128)(2,1)}), bf16[128,5120]{1,0:T(8,128)(2,1)}) %all-gather.9.cloned.1.call-update) | async-done | bytes 1310736 | tf_op jit(solution)/shard_map/all_gather | solution.py:57
  207.2 1.6 fusion.47
  208.9 8.3 %fusion.71 = f32[128,1792]{1,0:T(8,128)S(1)} fusion(bf16[2,5120,1792]{2,1,0:T(8,128)(2,1)} %param.19, bf16[128,5120]{1,0:T(8,128)(2,1)} %all-gather.9.cloned.1.call-done, f32[5120]{0:T(1024)S(1)} %bitcast.194, f32[128]{0:T(128)S(1)} %add_rsqrt_fusion), kind=kOutput, calls=%fused_computation.71 | convolution fusion | flops 2351890432 | bytes 20599296 | tf_op jit(solution)/shard_map/dot_general | solution.py:73
  217.2 8.0 %fusion.83 = bf16[128,1792]{1,0:T(8,128)(2,1)S(1)} fusion(bf16[2,5120,1792]{2,1,0:T(8,128)(2,1)} %param.20, f32[128,1792]{1,0:T(8,128)S(1)} %fusion.71, bf16[128,5120]{1,0:T(8,128)(2,1)S(1)} %copy-done.1, f32[5120]{0:T(1024)S(1)} %bitcast.195, f32[128]{0:T(128)S(1)} %add_rsqrt_fusion), kind=kOutput, calls=%fused_computation.75 | convolution fusion | flops 2353266688 | bytes 21058048 | tf_op jit(solution)/shard_map/dot_general | solution.py:74
  225.2 8.9 %fusion.27 = bf16[128,5120]{1,0:T(8,128)(2,1)S(1)} fusion(bf16[128,1792]{1,0:T(8,128)(2,1)S(1)} %fusion.83, bf16[2,1792,5120]{2,1,0:T(8,128)(2,1)} %param.21), kind=kOutput, calls=%fused_computation.25 | convolution fusion | flops 2349465600 | bytes 20119552 | tf_op jit(solution)/shard_map/dot_general | solution.py:76
  234.1 0.1 copy.95
  234.2 20.9 %all_to_all.22 = bf16[128,8,640]{2,0,1:T(8,128)(2,1)S(1)} all-to-all(bf16[128,8,640]{2,0,1:T(8,128)(2,1)S(1)} %bitcast.180), channel_id=1, replica_groups=mesh['dp'=2,'tp'=8] {'tp'}, dimensions={1} | all-to-all | bytes 2621440 | tf_op jit(solution)/shard_map/all_to_all | solution.py:54
  255.1 0.2 convert_reduce_fusion
  255.3 0.7 add_convert_fusion
  256.0 20.0 %all-gather.11.cloned.1.call-done = bf16[128,5120]{1,0:T(8,128)(2,1)} async-done(((bf16[128,640]{1,0:T(8,128)(2,1)}), bf16[128,5120]{1,0:T(8,128)(2,1)}) %all-gather.11.cloned.1.call-update) | async-done | bytes 1310736 | tf_op jit(solution)/shard_map/all_gather | solution.py:57
  276.0 2.5 copy.100
  (30 shorter events, 0.4 us)
Async XLA Ops:
  29.7 25.8 %copy-start.2 = (bf16[2,5120]{1,0:T(2,128)(2,1)S(1)}, bf16[2,5120]{1,0:T(2,128)(2,1)}, u32[]{:S(2)}) copy-start(bf16[2,5120]{1,0:T(2,128)(2,1)} %param.18) | copy-start | bytes 61444
  29.7 23.7 %all-to-all-start = ((bf16[128,8,640]{2,0,1:T(8,128)(2,1)}), bf16[128,8,640]{2,0,1:T(8,128)(2,1)S(1)}, u32[]{:S(2)}, u32[]{:S(2)}) async-start(bf16[128,8,640]{2,0,1:T(8,128)(2,1)} %bitcast.177), calls=%async_computation | async-start | bytes 2621440 | tf_op jit(solution)/shard_map/all_to_all | solution.py:54
  35.9 40.1 %all-gather.5.cloned.1.call-start = ((), (), s32[]{:S(2)}) async-start(), calls=%async_computation.4 | async-start | bytes 1474560 | tf_op jit(solution)/shard_map/all_gather | solution.py:57
  55.3 89.5 %all-gather.7.cloned.1.call-start = ((), (), s32[]{:S(2)}) async-start(), calls=%async_computation.5 | async-start | bytes 1474560 | tf_op jit(solution)/shard_map/all_gather | solution.py:57
  77.6 8.3 %copy-start = (bf16[128,5120]{1,0:T(8,128)(2,1)S(1)}, bf16[128,5120]{1,0:T(8,128)(2,1)}, u32[]{:S(2)}) copy-start(bf16[128,5120]{1,0:T(8,128)(2,1)} %all-gather.5.cloned.1.call-done) | copy-start | bytes 3932164
  124.8 82.4 %all-gather.9.cloned.1.call-start = ((), (), s32[]{:S(2)}) async-start(), calls=%async_computation.6 | async-start | bytes 1474560 | tf_op jit(solution)/shard_map/all_gather | solution.py:57
  187.2 88.8 %all-gather.11.cloned.1.call-start = ((), (), s32[]{:S(2)}) async-start(), calls=%async_computation.7 | async-start | bytes 1474560 | tf_op jit(solution)/shard_map/all_gather | solution.py:57
  208.9 8.3 %copy-start.1 = (bf16[128,5120]{1,0:T(8,128)(2,1)S(1)}, bf16[128,5120]{1,0:T(8,128)(2,1)}, u32[]{:S(2)}) copy-start(bf16[128,5120]{1,0:T(8,128)(2,1)} %all-gather.9.cloned.1.call-done) | copy-start | bytes 3932164
Sparse Core Ops, SparseCore 0:
  55.4 20.4 all-gather.4
  124.9 19.8 all-gather.6
  187.3 19.8 all-gather.8
  256.2 19.8 all-gather.10
where the time goes:
time: 286 us; the launch traced here: 285 us
  waiting for transfers between devices  97.5 us (34%)
  matrix products  83.4 us (29%)
  blocking collectives  62.6 us (22%)
  other arithmetic  15.9 us (6%)
  between operations  13.6 us (5%)
  starting transfers between devices  7.01 us (2%)
  local copies, waits for them, and re-layouts  5.05 us (2%)
    all_gather x4, waiting for transfers between devices, reduce_add(): return lax.all_gather(summed, 'tp', axis=1, tiled=True)  79.7 us
    all_to_all x3, blocking collectives, reduce_add(): lax.all_to_all(partial.reshape(rows, group_devs, width), 'tp', 1, 1, tile...  62.6 us
    dot_general x2, matrix products, local_step(): jnp.dot(activated, w_down[layer], preferred_element_type=jnp.float32)  17.8 us
    all_to_all x1, waiting for transfers between devices, reduce_add(): lax.all_to_all(partial.reshape(rows, group_devs, width), 'tp', 1, 1, tile...  17.6 us
    dot_general x2, matrix products, local_step(): jnp.dot(normed, w_gate[layer], preferred_element_type=jnp.float32)  16.6 us
    dot_general x2, matrix products, local_step(): jnp.dot(normed, w_up[layer], preferred_element_type=jnp.float32)  15.9 us
    dot_general x2, matrix products, local_step(): jnp.einsum('bd,dkf->bkf', normed, w_qkv[layer], preferred_element_type=jn...  9.8 us
    dot_general x2, matrix products, attention(): jnp.einsum('bkgd,bskd->bkgs', query, keys_layer, preferred_element_type=j...  9.08 us
  transfers between devices with their start and end apart: 5, of which 5 were waited for; matrix products, arithmetic and copies ran while one was open for 0% of the time, Pallas kernels for 0%

commit v1 on v0

v1 whole, which is shorter than its diff:
```python
import functools

import jax
import jax.numpy as jnp
from jax import lax
from jax.experimental import pallas as pl
from jax.experimental.pallas import tpu as pltpu
from jax.sharding import PartitionSpec as P

ROPE_BASE = 10000.0
NORM_EPS = 1e-5
F32 = jnp.float32
BF16 = jnp.bfloat16
MESH = pl.DeviceIdType.MESH
CORES = 2
GU_SLOTS = 5
DN_SLOTS = 2
NEG = -1e30


def rope_tables(lengths, head_dim):
    inv_freq = ROPE_BASE ** (-jnp.arange(0, head_dim, 2, dtype=F32) / head_dim)
    angles = lengths.astype(F32)[:, None] * inv_freq[None, :]
    cosine, sine = jnp.cos(angles), jnp.sin(angles)
    return jnp.concatenate([cosine, cosine], 1), jnp.concatenate([-sine, sine], 1)


def kernel(cfg, hid, lens, cos_ref, sin_ref, gain_attn, gain_mlp, wqkv, wout, wgate, wup, wdown, kc, vc, out,
           x, a_buf, rbuf, lrep, part, rel_in, prt_in, dir_in, own_in, f_out, f_in, stat,
           q_s, kn_s, vn_s, s_s, attn, act, g_acc, u_acc,
           b_qkv, b_out, b_k, b_v, b_gu, b_d,
           rs_sem, ag_sem, st_sem, snd_sem, snd2_sem, w_sem, x_sem):
    layers, rows, width, head_dim, group, chips, seq = cfg
    half = rows // 2
    wide = CORES * width
    qkv_cols = (group + 2) * head_dim
    d_model = chips * wide
    tp = lax.axis_index('tp')
    e = lax.rem(tp, CORES)
    c = lax.div(tp, CORES)
    other = 1 - e
    right = lax.rem(c + 1, chips)
    left = lax.rem(c + chips - 1, chips)
    far = lax.rem(c + 2, chips)
    first = pl.ds(0, half)
    second = pl.ds(half, half)

    def dev(chip, core):
        return {'tp': chip * CORES + core}

    def cols(chip):
        return pl.ds(pl.multiple_of(chip * wide, wide), wide)

    in_order = (c, left, right, far)
    out_order = (far, right, left, c)

    def ld_qkv(l, i):
        return pltpu.make_async_copy(wqkv.at[l, cols(in_order[i]), :], b_qkv.at[i], w_sem.at[i])

    def ld_out(l, i):
        return pltpu.make_async_copy(wout.at[l, :, cols(out_order[i])], b_out.at[i], w_sem.at[4 + i])

    def ld_k(l):
        return pltpu.make_async_copy(kc.at[l], b_k, w_sem.at[8])

    def ld_v(l):
        return pltpu.make_async_copy(vc.at[l], b_v, w_sem.at[9])

    def ld_gu(m):
        l, i, s = m // (2 * chips), m // 2 % chips, m % GU_SLOTS
        src = wup if m % 2 else wgate
        return pltpu.make_async_copy(src.at[l, cols(in_order[i]), :], b_gu.at[s], w_sem.at[10 + s])

    def ld_d(n):
        l, i, s = n // chips, n % chips, n % DN_SLOTS
        return pltpu.make_async_copy(wdown.at[l, :, cols(out_order[i])], b_d.at[s], w_sem.at[10 + GU_SLOTS + s])

    x_loads = [pltpu.make_async_copy(
        hid.at[:, pl.ds(k * wide + h * width, width)], x.at[k, h], x_sem.at[k, h])
        for k in range(chips) for h in range(CORES)]
    for cp in x_loads:
        cp.start()
    for i in range(chips):
        ld_qkv(0, i).start()
    ld_k(0).start()
    ld_v(0).start()
    for i in range(chips):
        ld_out(0, i).start()

    barrier = pltpu.get_barrier_semaphore()
    n_dev = chips * CORES
    for step in range(1, n_dev):
        pl.semaphore_signal(barrier, inc=1, device_id={'tp': lax.rem(tp + step, n_dev)}, device_id_type=MESH)
    pl.semaphore_wait(barrier, n_dev - 1)

    lens_row = jnp.broadcast_to(lens[...].astype(F32), (rows, rows)).T
    for g in range(group):
        lrep[pl.ds(g, rows, stride=group), :] = lens_row

    for cp in x_loads:
        cp.wait()
    total = jnp.zeros((rows, 128), F32)
    for k in range(chips):
        for h in range(CORES):
            for j in range(width // 128):
                v = x[k, h, :, j * 128:(j + 1) * 128].astype(F32)
                total = total + v * v
    scale0 = lax.rsqrt(jnp.sum(total, axis=1, keepdims=True) / d_model + NORM_EPS)
    rbuf[...] = jnp.broadcast_to(scale0, (rows, 128))

    def normed(chip, gain_ref, l):
        r = jnp.concatenate([rbuf[...]] * (width // 128), axis=1)
        gain = gain_ref[l:l + 1, cols(chip)].astype(F32)
        for h in range(CORES):
            piece = x[chip, h].astype(F32)
            a_buf[:, h * width:(h + 1) * width] = (
                piece * r * gain[:, h * width:(h + 1) * width]).astype(BF16)

    def use_qkv(l):
        def consume(i):
            normed(in_order[i], gain_attn, l)
            ld_qkv(l, i).wait()
            prod = jnp.dot(a_buf[...], b_qkv[i], preferred_element_type=F32)
            if i == 0:
                g_acc[:, :qkv_cols] = prod
            else:
                g_acc[:, :qkv_cols] += prod
            if l + 1 < layers:
                ld_qkv(l + 1, i).start()
        return consume

    def use_gu(l):
        def consume(i):
            normed(in_order[i], gain_mlp, l)
            for j, acc in enumerate((g_acc, u_acc)):
                m = 2 * (l * chips + i) + j
                ld_gu(m).wait()
                prod = jnp.dot(a_buf[...], b_gu[m % GU_SLOTS], preferred_element_type=F32)
                if i == 0:
                    acc[...] = prod
                else:
                    acc[...] += prod
                if m + GU_SLOTS < layers * chips * 2:
                    ld_gu(m + GU_SLOTS).start()
        return consume

    def attention(l):
        cosine, sine = cos_ref[...], sin_ref[...]

        def rot(v):
            return (v * cosine + pltpu.roll(v, head_dim // 2, 1) * sine).astype(BF16).astype(F32)

        def head(j):
            return g_acc[:, j * head_dim:(j + 1) * head_dim].astype(BF16).astype(F32)

        key_new = rot(head(group))
        val_new = head(group + 1)
        for g in range(group):
            at = pl.ds(g, rows, stride=group)
            q_s[at, :] = rot(head(g))
            kn_s[at, :] = key_new
            vn_s[at, :] = val_new
        scale = head_dim ** -0.5
        pair = 2 * group
        upper = lax.broadcasted_iota(jnp.int32, (pair, head_dim), 0) < group
        ld_k(l).wait()

        def scores(i, carry):
            at = pl.ds(pl.multiple_of(i * pair, pair), pair)
            q = q_s[at, :].astype(BF16)
            keys = b_k[pl.ds(i * 2, 2)].reshape(2 * seq, head_dim)
            s = lax.dot_general(q, keys, (((1,), (1,)), ((), ())), preferred_element_type=F32)
            s_s[at, :] = jnp.where(upper, s[:, :seq], s[:, seq:])
            return carry

        lax.fori_loop(0, rows // 2, scores, 0, unroll=8)
        if l + 1 < layers:
            ld_k(l + 1).start()
        pos = lax.broadcasted_iota(jnp.int32, (rows * group, seq), 1).astype(F32)
        s = jnp.where(pos < lrep[...], s_s[...] * scale, NEG)
        own = jnp.sum(q_s[...] * kn_s[...], axis=1, keepdims=True) * scale
        peak = jnp.maximum(jnp.max(s, axis=1, keepdims=True), own)
        w = jnp.exp(s - peak).astype(BF16).astype(F32)
        w_own = jnp.exp(own - peak).astype(BF16).astype(F32)
        denom = jnp.sum(w, axis=1, keepdims=True) + w_own
        s_s[...] = w
        q_s[...] = w_own * vn_s[...]
        kn_s[...] = jnp.broadcast_to(denom, kn_s.shape)
        ld_v(l).wait()

        def mix(i, carry):
            at = pl.ds(pl.multiple_of(i * pair, pair), pair)
            w = s_s[at, :].astype(BF16)
            vals = jnp.concatenate([b_v[i * 2], b_v[i * 2 + 1]], axis=1)
            o = jnp.dot(w, vals, preferred_element_type=F32)
            o = jnp.where(upper, o[:, :head_dim], o[:, head_dim:])
            s_s[at, :] = (o + q_s[at, :]) / kn_s[at, :]
            return carry

        lax.fori_loop(0, rows // 2, mix, 0, unroll=8)
        if l + 1 < layers:
            ld_v(l + 1).start()
        for g in range(group):
            attn[:, g * head_dim:(g + 1) * head_dim] = s_s[pl.ds(g, rows, stride=group), :].astype(BF16)

    def chunk_out(l):
        def chunk(i):
            ld_out(l, i).wait()
            prod = jnp.dot(attn[...], b_out[i], preferred_element_type=F32)
            part[i, 0] = prod[:, :width].astype(BF16)
            part[i, 1] = prod[:, width:].astype(BF16)
            if l + 1 < layers:
                ld_out(l + 1, i).start()
        return chunk

    def chunk_down(l):
        def chunk(i):
            n = l * chips + i
            ld_d(n).wait()
            prod = jnp.dot(act[...], b_d[n % DN_SLOTS], preferred_element_type=F32)
            part[i, 0] = prod[:, :width].astype(BF16)
            part[i, 1] = prod[:, width:].astype(BF16)
            if n + DN_SLOTS < layers * chips:
                ld_d(n + DN_SLOTS).start()
        return chunk

    def reduce_scatter(chunk):
        sends = []

        def send(src, dst, rsem, where):
            cp = pltpu.make_async_remote_copy(
                src_ref=src, dst_ref=dst, send_sem=snd_sem.at[len(sends)], recv_sem=rsem,
                device_id=where, device_id_type=MESH)
            cp.start()
            sends.append(cp)

        def arrived(dst, rsem):
            pltpu.make_async_remote_copy(
                src_ref=dst, dst_ref=dst, send_sem=snd_sem.at[0], recv_sem=rsem,
                device_id=dev(c, e), device_id_type=MESH).wait_recv()

        chunk(0)
        for q in range(CORES):
            send(part.at[0, q, first], rel_in.at[0, e], rs_sem.at[e], dev(right, q))
            send(part.at[0, q, second], rel_in.at[1, e], rs_sem.at[2 + e], dev(left, q))
        chunk(1)
        send(part.at[1, other, first], prt_in.at[0], rs_sem.at[4], dev(c, other))
        for q in range(CORES):
            send(part.at[1, q, second], dir_in.at[1, e], rs_sem.at[8 + e], dev(right, q))
        chunk(2)
        send(part.at[2, other, second], prt_in.at[1], rs_sem.at[5], dev(c, other))
        for q in range(CORES):
            send(part.at[2, q, first], dir_in.at[0, e], rs_sem.at[6 + e], dev(left, q))
        chunk(3)
        send(part.at[3, other], own_in, rs_sem.at[12], dev(c, other))
        for way in range(2):
            where = (first, second)[way]
            for q in range(CORES):
                arrived(rel_in.at[way, q], rs_sem.at[2 * way + q])
            arrived(prt_in.at[way], rs_sem.at[4 + way])
            f_out[way] = (rel_in[way, 0].astype(F32) + rel_in[way, 1].astype(F32)
                          + (prt_in[way].astype(F32) + part[1 + way, e, where].astype(F32)))
            send(f_out.at[way], f_in.at[way], rs_sem.at[10 + way], dev((right, left)[way], e))
        arrived(own_in, rs_sem.at[12])
        squares = []
        for way in range(2):
            where = (first, second)[way]
            for q in range(CORES):
                arrived(dir_in.at[way, q], rs_sem.at[6 + 2 * way + q])
            arrived(f_in.at[way], rs_sem.at[10 + way])
            h = ((part[3, e, where].astype(F32) + own_in[where].astype(F32))
                 + (dir_in[way, 0].astype(F32) + dir_in[way, 1].astype(F32)) + f_in[way])
            h = (x[c, e, where].astype(F32) + h).astype(BF16)
            x[c, e, where] = h
            h = h.astype(F32)
            sq = h * h
            tot = sq[:, :128]
            for j in range(1, width // 128):
                tot = tot + sq[:, j * 128:(j + 1) * 128]
            squares.append(tot)
        for cp in sends:
            cp.wait_send()
        return jnp.concatenate(squares, axis=0)

    def all_gather(squares, consume):
        sends = []

        def send(src, dst, rsem, where):
            cp = pltpu.make_async_remote_copy(
                src_ref=src, dst_ref=dst, send_sem=snd2_sem.at[len(sends)], recv_sem=rsem,
                device_id=where, device_id_type=MESH)
            cp.start()
            sends.append(cp)

        def arrived(dst, rsem):
            pltpu.make_async_remote_copy(
                src_ref=dst, dst_ref=dst, send_sem=snd2_sem.at[0], recv_sem=rsem,
                device_id=dev(c, e), device_id_type=MESH).wait_recv()

        ranges = (first, second)

        def push(chip, core, way, where):
            ref = x.at[chip, core, ranges[way]]
            send(ref, ref, ag_sem.at[chip, core, way], where)

        def have(chip, core, way):
            arrived(x.at[chip, core, ranges[way]], ag_sem.at[chip, core, way])

        if squares is not None:
            row = jnp.sum(squares.T, axis=0, keepdims=True)
            stat[tp] = jnp.broadcast_to(row, (8, rows))
            for step in range(1, n_dev):
                send(stat.at[tp], stat.at[tp], st_sem.at[tp], {'tp': lax.rem(tp + step, n_dev)})
        push(c, e, 0, dev(right, e))
        push(c, e, 1, dev(left, e))
        push(c, e, 1, dev(right, e))
        push(c, e, 0, dev(left, e))
        push(c, e, 0, dev(c, other))
        push(c, e, 1, dev(c, other))
        if squares is not None:
            for step in range(1, n_dev):
                src = lax.rem(tp + step, n_dev)
                arrived(stat.at[src], st_sem.at[src])
            row = stat[0, 0:1]
            for j in range(1, n_dev):
                row = row + stat[j, 0:1]
            rbuf[...] = jnp.broadcast_to(lax.rsqrt(row / d_model + NORM_EPS), (rows, rows)).T
        have(c, other, 0)
        have(c, other, 1)
        consume(0)
        have(left, e, 0)
        push(left, e, 0, dev(right, e))
        push(left, e, 0, dev(c, other))
        have(right, e, 1)
        push(right, e, 1, dev(left, e))
        push(right, e, 1, dev(c, other))
        have(left, e, 1)
        push(left, e, 1, dev(c, other))
        have(right, e, 0)
        push(right, e, 0, dev(c, other))
        have(left, other, 0)
        have(left, other, 1)
        consume(1)
        have(far, e, 0)
        push(far, e, 0, dev(c, other))
        have(far, e, 1)
        push(far, e, 1, dev(c, other))
        have(right, other, 0)
        have(right, other, 1)
        consume(2)
        have(far, other, 0)
        have(far, other, 1)
        consume(3)
        for cp in sends:
            cp.wait_send()

    for i in range(chips):
        use_qkv(0)(i)
    for m in range(GU_SLOTS):
        ld_gu(m).start()
    for l in range(layers):
        attention(l)
        if l == 0:
            for n in range(DN_SLOTS):
                ld_d(n).start()
        squares = reduce_scatter(chunk_out(l))
        all_gather(squares, use_gu(l))
        gate = g_acc[...].astype(BF16).astype(F32)
        up = u_acc[...].astype(BF16).astype(F32)
        act[...] = (gate * jax.nn.sigmoid(gate) * up).astype(BF16)
        squares = reduce_scatter(chunk_down(l))
        if l + 1 < layers:
            all_gather(squares, use_qkv(l + 1))
    stores = []

    def store(i):
        for h in range(CORES):
            cp = pltpu.make_async_copy(
                x.at[in_order[i], h],
                out.at[:, pl.ds(pl.multiple_of(in_order[i] * wide + h * width, width), width)],
                x_sem.at[i, h])
            cp.start()
            stores.append(cp)

    all_gather(None, store)
    for cp in stores:
        cp.wait()


def solution(mesh):
    n_dev = mesh.shape['tp']
    chips = n_dev // CORES

    def local_step(hidden, lengths, k_cache, v_cache, attn_norm, w_qkv, w_out, mlp_norm, w_gate, w_up, w_down):
        layers, rows, seq, _, head_dim = k_cache.shape
        d_model = hidden.shape[1]
        width = d_model // n_dev
        qkv_cols = w_qkv.shape[3]
        group = qkv_cols // head_dim - 2
        ff = w_gate.shape[2]
        half = rows // 2
        wide = CORES * width
        heads = group * head_dim
        cosine, sine = rope_tables(lengths, head_dim)
        cfg = (layers, rows, width, head_dim, group, chips, seq)
        vmem = pl.BlockSpec(memory_space=pltpu.VMEM)
        hbm = pl.BlockSpec(memory_space=pl.ANY)
        flops = 2 * layers * rows * d_model * (qkv_cols + heads + 3 * ff)
        return pl.pallas_call(
            functools.partial(kernel, cfg),
            out_shape=jax.ShapeDtypeStruct((rows, d_model), BF16),
            in_specs=[hbm] + [vmem] * 5 + [hbm] * 7,
            out_specs=hbm,
            scratch_shapes=[
                pltpu.VMEM((chips, CORES, rows, width), BF16),
                pltpu.VMEM((rows, wide), BF16),
                pltpu.VMEM((rows, 128), F32),
                pltpu.VMEM((rows * group, seq), F32),
                pltpu.VMEM((chips, CORES, rows, width), BF16),
                pltpu.VMEM((2, CORES, half, width), BF16),
                pltpu.VMEM((2, half, width), BF16),
                pltpu.VMEM((2, CORES, half, width), BF16),
                pltpu.VMEM((rows, width), BF16),
                pltpu.VMEM((2, half, width), F32),
                pltpu.VMEM((2, half, width), F32),
                pltpu.VMEM((n_dev, 8, rows), F32),
                pltpu.VMEM((rows * group, head_dim), F32),
                pltpu.VMEM((rows * group, head_dim), F32),
                pltpu.VMEM((rows * group, head_dim), F32),
                pltpu.VMEM((rows * group, seq), F32),
                pltpu.VMEM((rows, heads), BF16),
                pltpu.VMEM((rows, ff), BF16),
                pltpu.VMEM((rows, ff), F32),
                pltpu.VMEM((rows, ff), F32),
                pltpu.VMEM((chips, wide, qkv_cols), BF16),
                pltpu.VMEM((chips, heads, wide), BF16),
                pltpu.VMEM((rows, seq, head_dim), BF16),
                pltpu.VMEM((rows, seq, head_dim), BF16),
                pltpu.VMEM((GU_SLOTS, wide, ff), BF16),
                pltpu.VMEM((DN_SLOTS, ff, wide), BF16),
                pltpu.SemaphoreType.DMA((13,)),
                pltpu.SemaphoreType.DMA((chips, CORES, 2)),
                pltpu.SemaphoreType.DMA((n_dev,)),
                pltpu.SemaphoreType.DMA((16,)),
                pltpu.SemaphoreType.DMA((24,)),
                pltpu.SemaphoreType.DMA((10 + GU_SLOTS + DN_SLOTS,)),
                pltpu.SemaphoreType.DMA((chips, CORES)),
            ],
            compiler_params=pltpu.CompilerParams(
                collective_id=0, has_side_effects=True, vmem_limit_bytes=67043328),
            cost_estimate=pl.CostEstimate(flops=flops, bytes_accessed=flops // rows, transcendentals=0),
        )(hidden, lengths.reshape(1, rows), cosine, sine, attn_norm, mlp_norm,
          w_qkv.reshape(layers, d_model, qkv_cols), w_out, w_gate, w_up, w_down,
          k_cache.reshape(layers, rows, seq, head_dim), v_cache.reshape(layers, rows, seq, head_dim))

    cache_spec = P(None, 'dp', None, 'tp', None)
    in_specs = (P('dp', None), P('dp'), cache_spec, cache_spec, P(), P(None, None, 'tp', None),
                P(None, 'tp', None), P(), P(None, None, 'tp'), P(None, None, 'tp'), P(None, 'tp', None))
    return jax.shard_map(local_step, mesh=mesh, in_specs=in_specs, out_specs=P('dp', None), check_vma=False)
```

time: 286 us -> 129 us (0.45)
  Pallas kernels: 0 us -> 124 us
  waiting for transfers between devices: 97.5 us -> 0 us
  matrix products: 83.4 us -> 0 us
  blocking collectives: 62.6 us -> 0 us
  other arithmetic: 15.9 us -> 1.73 us
  between operations: 13.6 us -> 0.02 us
  starting transfers between devices: 7.01 us -> 0 us
    pallas_call x0 -> x1, Pallas kernels: none -> 124 us  [local_step(): pl.pallas_call(functools.partial(kernel, cfg), out_shape=jax.ShapeDtypeSt...]
    dot_general x16 -> x0, matrix products: 83.4 us -> none  [the longest x2 17.8 us: local_step(): jnp.dot(activated, w_down[layer], preferred_element_type=jnp.float32)]
    all_gather x4 -> x0, waiting for transfers between devices: 79.7 us -> none  [reduce_add(): return lax.all_gather(summed, 'tp', axis=1, tiled=True)]
    all_to_all x3 -> x0, blocking collectives: 62.6 us -> none  [reduce_add(): lax.all_to_all(partial.reshape(rows, group_devs, width), 'tp', 1, 1, tile...]
    all_to_all x1 -> x0, waiting for transfers between devices: 17.6 us -> none  [reduce_add(): lax.all_to_all(partial.reshape(rows, group_devs, width), 'tp', 1, 1, tile...]
    reduce_sum x10 -> x0, other arithmetic: 8.05 us -> none  [the longest x4 6.6 us: rms_norm(): scale = lax.rsqrt(jnp.mean(wide * wide, axis=-1, keepdims=True) + NORM_EPS)]
    all_to_all x1 -> x0, starting transfers between devices: 6.15 us -> none  [reduce_add(): lax.all_to_all(partial.reshape(rows, group_devs, width), 'tp', 1, 1, tile...]
    convert_element_type x7 -> x1, other arithmetic: 5.4 us -> 0.66 us  [rope_tables(): angles = lengths.astype(F32)[:, None] * inv_freq[None, :]]
  transfers between devices with their start and end apart: 5 -> 0, of which waited for: 5 -> 0; matrix products, arithmetic and copies ran while one was open for 0% -> 0% of each run, Pallas kernels for 0% -> 0%
where the time goes in v1:
time: 129 us; the launch traced here: 128 us
  Pallas kernels  124 us (96%)
  local copies, waits for them, and re-layouts  2.46 us (2%)
  other arithmetic  1.73 us (1%)
    pallas_call x1, Pallas kernels, local_step(): pl.pallas_call(functools.partial(kernel, cfg), out_shape=jax.ShapeDtypeSt...  124 us

profile of v1, /device:TPU:113, one launch (start us, length us, event | category | flops | bytes accessed | tf_op | source)
XLA Modules:
  0.0 128.4 jit_solution(12013243808626460438)
XLA Ops:
  0.0 0.7 convert_element_type.3
  0.7 0.3 fusion
  1.0 0.7 pad_maximum_fusion
  1.7 124.2 %shard_map.109 = bf16[128,5120]{1,0:T(8,128)(2,1)} custom-call(bf16[128,5120]{1,0:T(8,128)(2,1)} %hid.1, s32[1,128]{1,0:T(1,128)} %bitcast.7, f32[128,128]{1,0:T(8,128)} %get-tuple-element.8.cos_ref, f32[128,128]{1,0:T(8,128)} %get-tuple-element.9.sin_ref, bf16[2,5120]{1,0:T(2,128)(2,1)} %gain_attn.1, bf16[2,5120]{1,0:T(2,128)(2,1)} %gain_mlp.1, ...), custom_call_target="tpu_custom_call" | custom-call | flops 17448304640 | bytes 136314880 | tf_op jit(solution)/shard_map/pallas_call | solution.py:409
  125.9 2.5 %copy.13 = bf16[128,5120]{1,0:T(8,128)(2,1)} copy(bf16[128,5120]{1,0:T(8,128)(2,1)} %shard_map.109) | data formatting | bytes 2621440
  (1 shorter events, 0.0 us)

commit v2 on v0

v2 whole, which is shorter than its diff:
```python
import functools

import jax
import jax.numpy as jnp
from jax import lax
from jax.experimental import pallas as pl
from jax.experimental.pallas import tpu as pltpu
from jax.sharding import PartitionSpec as P

ROPE_BASE = 10000.0
NORM_EPS = 1e-5
F32 = jnp.float32
BF16 = jnp.bfloat16
MESH = pl.DeviceIdType.MESH
CORES = 2
HALVES = 2
NEG = -1e30


def rope_tables(lengths, head_dim):
    inv_freq = ROPE_BASE ** (-jnp.arange(0, head_dim, 2, dtype=F32) / head_dim)
    angles = lengths.astype(F32)[:, None] * inv_freq[None, :]
    cosine, sine = jnp.cos(angles), jnp.sin(angles)
    return jnp.concatenate([cosine, cosine], 1), jnp.concatenate([-sine, sine], 1)


def kernel(cfg, hid, lens, cos_ref, sin_ref, gain_attn, gain_mlp, wqkv, wout, wgate, wup, wdown, kc, vc, out,
           x, a_buf, rbuf, lrep, part, rel_in, prt_in, dir_in, own_in, f_out, f_in, stat,
           q_s, kn_s, vn_s, s_s, attn, act, g_acc, u_acc, b_g, b_u, b_d, b_v,
           rs_sem, ag_sem, st_sem, snd_sem, snd2_sem, w_sem, k_sem, g_sem, x_sem):
    layers, rows, width, head_dim, group, chips, seq = cfg
    part_rows = rows // HALVES
    quart = part_rows // 2
    wide = CORES * width
    qkv_cols = (group + 2) * head_dim
    heads = group * head_dim
    d_model = chips * wide
    n_dev = chips * CORES
    tp = lax.axis_index('tp')
    e = lax.rem(tp, CORES)
    c = lax.div(tp, CORES)
    other = 1 - e
    right = lax.rem(c + 1, chips)
    left = lax.rem(c + chips - 1, chips)
    far = lax.rem(c + 2, chips)
    in_order = (c, left, right, far)
    out_order = (far, right, left, c)
    ways = (pl.ds(0, quart), pl.ds(quart, quart))

    def half_rows(h):
        return pl.ds(h * part_rows, part_rows)

    def way_rows(h, way):
        return pl.ds(h * part_rows + way * quart, quart)

    def dev(chip, core):
        return {'tp': chip * CORES + core}

    def when(cond, body):
        if cond is True:
            body()
        elif cond is not False:
            pl.when(cond)(body)

    def cols(chip):
        return pl.ds(pl.multiple_of(chip * wide, wide), wide)

    def qkv_at(i):
        return b_d.at[i, 0:wide, 0:qkv_cols]

    def out_at(i):
        return b_d.at[i, wide:wide + heads, :]

    per_block = wide // seq
    lane_blocks = (wide - qkv_cols) // head_dim
    n_blocks = -(-rows // per_block)

    def key_at(j, first_row, n):
        lane = qkv_cols + (j % lane_blocks) * head_dim
        return b_d.at[j // lane_blocks, first_row:first_row + n, lane:lane + head_dim]

    def ld_qkv(l, i):
        return pltpu.make_async_copy(wqkv.at[l, cols(in_order[i]), :], qkv_at(i), w_sem.at[i])

    def ld_out(l, i):
        return pltpu.make_async_copy(wout.at[l, :, cols(out_order[i])], out_at(i), w_sem.at[4 + i])

    def ld_k(l, j):
        n = min(per_block, rows - j * per_block) * seq
        return pltpu.make_async_copy(kc.at[l, pl.ds(j * wide, n), :], key_at(j, 0, n), k_sem.at[j])

    def ld_v(l):
        return pltpu.make_async_copy(vc.at[l], b_v, w_sem.at[12])

    def ld_g(l, i):
        return pltpu.make_async_copy(wgate.at[l, cols(in_order[i]), :], b_g.at[i], g_sem.at[i])

    def ld_u(l, i):
        return pltpu.make_async_copy(wup.at[l, cols(in_order[i]), :], b_u.at[i], g_sem.at[chips + i])

    def ld_d(l, i):
        return pltpu.make_async_copy(wdown.at[l, :, cols(out_order[i])], b_d.at[i], w_sem.at[8 + i])

    def start_keys(l, slots):
        for j in range(n_blocks):
            if j // lane_blocks in slots:
                ld_k(l, j).start()

    x_loads = [pltpu.make_async_copy(
        hid.at[:, pl.ds(k * wide + h * width, width)], x.at[k, h], x_sem.at[k, h])
        for k in range(chips) for h in range(CORES)]
    for cp in x_loads:
        cp.start()
    for i in range(chips):
        ld_qkv(0, i).start()
    start_keys(0, range(chips))
    ld_v(0).start()
    for i in range(chips):
        ld_out(0, i).start()

    barrier = pltpu.get_barrier_semaphore()
    for step in range(1, n_dev):
        pl.semaphore_signal(barrier, inc=1, device_id={'tp': lax.rem(tp + step, n_dev)}, device_id_type=MESH)
    pl.semaphore_wait(barrier, n_dev - 1)

    lens_row = jnp.broadcast_to(lens[...].astype(F32), (rows, rows)).T
    for g in range(group):
        lrep[pl.ds(g, rows, stride=group), :] = lens_row

    for cp in x_loads:
        cp.wait()
    total = jnp.zeros((rows, 128), F32)
    for k in range(chips):
        for h in range(CORES):
            for j in range(width // 128):
                v = x[k, h, :, j * 128:(j + 1) * 128].astype(F32)
                total = total + v * v
    scale0 = lax.rsqrt(jnp.sum(total, axis=1, keepdims=True) / d_model + NORM_EPS)
    rbuf[...] = jnp.broadcast_to(scale0, (rows, 128))

    def normed(chip, gain_ref, l, h):
        r = jnp.concatenate([rbuf[half_rows(h), :]] * (width // 128), axis=1)
        gain = gain_ref[0:1, cols(chip)].astype(F32)
        for k in range(1, layers):
            gain = jnp.where(l == k, gain_ref[k:k + 1, cols(chip)].astype(F32), gain)
        for q in range(CORES):
            piece = x[chip, q, half_rows(h)].astype(F32)
            a_buf[:, q * width:(q + 1) * width] = (
                piece * r * gain[:, q * width:(q + 1) * width]).astype(BF16)

    def accumulate(acc, prod, i):
        if i == 0:
            acc[...] = prod
        else:
            acc[...] += prod

    def use_qkv(l, h):
        def use(i):
            normed(in_order[i], gain_attn, l, h)
            if h == 0:
                ld_qkv(l, i).wait()
            prod = jnp.dot(a_buf[...], qkv_at(i)[...], preferred_element_type=F32)
            accumulate(g_acc.at[:, 0:qkv_cols], prod, i)
        return use

    def use_gu(l, h):
        def use(i):
            normed(in_order[i], gain_mlp, l, h)
            for ld, buf, acc in ((ld_g, b_g, g_acc), (ld_u, b_u, u_acc)):
                if h == 0:
                    ld(l, i).wait()
                accumulate(acc, jnp.dot(a_buf[...], buf[i], preferred_element_type=F32), i)
                if h == 1 and i < 2:
                    when(l + 1 < layers, lambda: ld(l + 1, i).start())
        return use

    def attention(l, h):
        cosine, sine = cos_ref[half_rows(h), :], sin_ref[half_rows(h), :]

        def rot(v):
            return (v * cosine + pltpu.roll(v, head_dim // 2, 1) * sine).astype(BF16).astype(F32)

        def head(j):
            return g_acc[:, j * head_dim:(j + 1) * head_dim].astype(BF16).astype(F32)

        key_new = rot(head(group))
        val_new = head(group + 1)
        for g in range(group):
            at = pl.ds(g, part_rows, stride=group)
            q_s[at, :] = rot(head(g))
            kn_s[at, :] = key_new
            vn_s[at, :] = val_new
        scale = head_dim ** -0.5
        pair = 2 * group
        upper = lax.broadcasted_iota(jnp.int32, (pair, head_dim), 0) < group
        if h == 0:
            for j in range(n_blocks):
                ld_k(l, j).wait()
        for p in range(part_rows // 2):
            at = slice(p * pair, (p + 1) * pair)
            b = h * part_rows + 2 * p
            keys = key_at(b // per_block, b % per_block * seq, 2 * seq)[...]
            s = lax.dot_general(q_s[at, :].astype(BF16), keys, (((1,), (1,)), ((), ())),
                                preferred_element_type=F32)
            s_s[at, :] = jnp.where(upper, s[:, :seq], s[:, seq:])
        pos = lax.broadcasted_iota(jnp.int32, (part_rows * group, seq), 1).astype(F32)
        live = pos < lrep[h * part_rows * group:(h + 1) * part_rows * group, :]
        s = jnp.where(live, s_s[...] * scale, NEG)
        own = jnp.sum(q_s[...] * kn_s[...], axis=1, keepdims=True) * scale
        peak = jnp.maximum(jnp.max(s, axis=1, keepdims=True), own)
        w = jnp.exp(s - peak).astype(BF16).astype(F32)
        w_own = jnp.exp(own - peak).astype(BF16).astype(F32)
        denom = jnp.sum(w, axis=1, keepdims=True) + w_own
        s_s[...] = w
        q_s[...] = w_own * vn_s[...]
        kn_s[...] = jnp.broadcast_to(denom, kn_s.shape)
        if h == 0:
            ld_v(l).wait()
        for p in range(part_rows // 2):
            at = slice(p * pair, (p + 1) * pair)
            b = h * part_rows + 2 * p
            vals = jnp.concatenate([b_v[b], b_v[b + 1]], axis=1)
            o = jnp.dot(s_s[at, :].astype(BF16), vals, preferred_element_type=F32)
            o = jnp.where(upper, o[:, :head_dim], o[:, head_dim:])
            s_s[at, :] = (o + q_s[at, :]) / kn_s[at, :]
        if h == 1:
            when(l + 1 < layers, lambda: ld_v(l + 1).start())
        for g in range(group):
            attn[:, g * head_dim:(g + 1) * head_dim] = s_s[pl.ds(g, part_rows, stride=group), :].astype(BF16)

    def activate():
        gate = g_acc[...].astype(BF16).astype(F32)
        up = u_acc[...].astype(BF16).astype(F32)
        act[...] = (gate * jax.nn.sigmoid(gate) * up).astype(BF16)

    def put_part(h, i, prod):
        part[h, i, 0] = prod[:, :width].astype(BF16)
        part[h, i, 1] = prod[:, width:].astype(BF16)

    def chunk_out(l, h):
        def chunk(i):
            if h == 0:
                ld_out(l, i).wait()
            put_part(h, i, jnp.dot(attn[...], out_at(i)[...], preferred_element_type=F32))
            if h == 1:
                ld_d(l, i).start()
        return chunk

    def chunk_down(l, h):
        def chunk(i):
            if h == 0:
                ld_d(l, i).wait()
            put_part(h, i, jnp.dot(act[...], b_d[i], preferred_element_type=F32))
            if h == 1:
                def nxt():
                    ld_qkv(l + 1, i).start()
                    start_keys(l + 1, (i,))
                    if i == chips - 1:
                        for k in range(chips):
                            ld_out(l + 1, k).start()
                        for k in range(2, chips):
                            ld_g(l + 1, k).start()
                            ld_u(l + 1, k).start()
                when(l + 1 < layers, nxt)
        return chunk

    def remote(src, dst, ssem, rsem, where):
        return pltpu.make_async_remote_copy(
            src_ref=src, dst_ref=dst, send_sem=ssem, recv_sem=rsem, device_id=where, device_id_type=MESH)

    me = dev(c, e)

    def arrived(dst, rsem):
        remote(dst, dst, rsem, rsem, me).wait_recv()

    def sent(src, ssem):
        remote(src, src, ssem, ssem, me).wait_send()

    def scatter_sends(h, i):
        if i == 0:
            return [(part.at[h, 0, q, ways[w]], rel_in.at[h, w, e], rs_sem.at[h, 2 * w + e],
                     dev((right, left)[w], q)) for q in range(CORES) for w in range(2)]
        if i in (1, 2):
            w = i - 1
            hop = (right, left)[w]
            return [(part.at[h, i, other, ways[w]], prt_in.at[h, w], rs_sem.at[h, 4 + w], dev(c, other))] + [
                (part.at[h, i, q, ways[1 - w]], dir_in.at[h, 1 - w, e], rs_sem.at[h, 6 + 2 * (1 - w) + e],
                 dev(hop, q)) for q in range(CORES)]
        if i == 3:
            return [(part.at[h, 3, other], own_in.at[h], rs_sem.at[h, 12], dev(c, other))]
        w = i - 4
        return [(f_out.at[h, w], f_in.at[h, w], rs_sem.at[h, 10 + w], dev((right, left)[w], e))]

    scatter_base = (0, 4, 7, 10, 11, 12)

    def scatter(h, i):
        for n, (src, dst, rsem, where) in enumerate(scatter_sends(h, i)):
            remote(src, dst, snd_sem.at[h, scatter_base[i] + n], rsem, where).start()

    def relay(h):
        for w in range(2):
            for q in range(CORES):
                arrived(rel_in.at[h, w, q], rs_sem.at[h, 2 * w + q])
            arrived(prt_in.at[h, w], rs_sem.at[h, 4 + w])
            f_out[h, w] = (rel_in[h, w, 0].astype(F32) + rel_in[h, w, 1].astype(F32)
                           + (prt_in[h, w].astype(F32) + part[h, 1 + w, e, ways[w]].astype(F32)))
            scatter(h, 4 + w)

    def gather_sends(h, group_id):
        def push(chip, core, w, where):
            ref = x.at[chip, core, way_rows(h, w)]
            return ref, ref, ag_sem.at[h, chip, core, w], where
        mate = dev(c, other)
        if group_id == 0:
            return [(stat.at[h, tp], stat.at[h, tp], st_sem.at[h, tp], {'tp': lax.rem(tp + step, n_dev)})
                    for step in range(1, n_dev)]
        if group_id == 1:
            return [push(c, e, 0, dev(right, e)), push(c, e, 1, dev(left, e)),
                    push(c, e, 1, dev(right, e)), push(c, e, 0, dev(left, e)),
                    push(c, e, 0, mate), push(c, e, 1, mate)]
        if group_id == 2:
            return [push(left, e, 0, dev(right, e)), push(left, e, 0, mate)]
        if group_id == 3:
            return [push(right, e, 1, dev(left, e)), push(right, e, 1, mate)]
        if group_id == 4:
            return [push(left, e, 1, mate)]
        if group_id == 5:
            return [push(right, e, 0, mate)]
        return [push(far, e, 0, mate), push(far, e, 1, mate)]

    gather_base = (0, 7, 13, 15, 17, 18, 19)

    def gather(h, i):
        for n, (src, dst, rsem, where) in enumerate(gather_sends(h, i)):
            remote(src, dst, snd2_sem.at[h, gather_base[i] + n], rsem, where).start()

    def gather_done(h, with_stats):
        for i in range(0 if with_stats else 1, 7):
            for n, (src, dst, rsem, where) in enumerate(gather_sends(h, i)):
                sent(src, snd2_sem.at[h, gather_base[i] + n])

    def have(h, chip, core, w):
        arrived(x.at[chip, core, way_rows(h, w)], ag_sem.at[h, chip, core, w])

    def have_both(h, chip, core):
        have(h, chip, core, 0)
        have(h, chip, core, 1)

    def finish_sum(h, with_stats):
        arrived(own_in.at[h], rs_sem.at[h, 12])
        squares = []
        for w in range(2):
            for q in range(CORES):
                arrived(dir_in.at[h, w, q], rs_sem.at[h, 6 + 2 * w + q])
            arrived(f_in.at[h, w], rs_sem.at[h, 10 + w])
            v = ((part[h, 3, e, ways[w]].astype(F32) + own_in[h, ways[w]].astype(F32))
                 + (dir_in[h, w, 0].astype(F32) + dir_in[h, w, 1].astype(F32)) + f_in[h, w])
            v = (x[c, e, way_rows(h, w)].astype(F32) + v).astype(BF16)
            x[c, e, way_rows(h, w)] = v
            v = v.astype(F32)
            sq = v * v
            tot = sq[:, :128]
            for j in range(1, width // 128):
                tot = tot + sq[:, j * 128:(j + 1) * 128]
            squares.append(tot)
        gather(h, 1)
        if with_stats:
            row = jnp.sum(jnp.concatenate(squares * HALVES, axis=0).T, axis=0, keepdims=True)
            stat[h, tp] = jnp.broadcast_to(row, (8, rows))
            gather(h, 0)
        for i in range(6):
            for n, (src, dst, rsem, where) in enumerate(scatter_sends(h, i)):
                sent(src, snd_sem.at[h, scatter_base[i] + n])

    def forward(h, with_stats):
        have(h, left, e, 0)
        gather(h, 2)
        have(h, right, e, 1)
        gather(h, 3)
        if with_stats:
            for step in range(1, n_dev):
                src = lax.rem(tp + step, n_dev)
                arrived(stat.at[h, src], st_sem.at[h, src])
            row = stat[h, 0, 0:1]
            for j in range(1, n_dev):
                row = row + stat[h, j, 0:1]
            r = jnp.broadcast_to(lax.rsqrt(row / d_model + NORM_EPS), (rows, rows)).T
            rbuf[half_rows(h), :] = r[:part_rows]
        have(h, left, e, 1)
        gather(h, 4)
        have(h, right, e, 0)
        gather(h, 5)
        have_both(h, c, other)

    def forward_far(h):
        have_both(h, far, e)
        gather(h, 6)

    def window(producing, p, chunk, gathered, h, use, finish, next_chunk, with_stats=True,
               sum_stats=True):
        def rest():
            for i in range(1, chips):
                chunk(i)
                scatter(p, i)
        when(producing, rest)
        when(gathered, lambda: forward(h, with_stats))
        use(0)
        when(producing, lambda: relay(p))
        when(gathered, lambda: have_both(h, left, other))
        use(1)

        def mid():
            forward_far(h)
            have_both(h, right, other)
        when(gathered, mid)
        use(2)
        when(gathered, lambda: have_both(h, far, other))
        use(3)
        when(gathered, lambda: gather_done(h, with_stats))
        finish()
        when(producing, lambda: finish_sum(p, sum_stats))
        if next_chunk is not None:
            next_chunk(0)
            scatter(h, 0)

    def layer(l, carry):
        later = l > 0
        window(later, 1, chunk_down(l - 1, 1), later, 0, use_qkv(l, 0), lambda: attention(l, 0), chunk_out(l, 0))

        def first_gu():
            for i in range(chips):
                ld_g(0, i).start()
                ld_u(0, i).start()
        when(l == 0, first_gu)
        window(True, 0, chunk_out(l, 0), later, 1, use_qkv(l, 1), lambda: attention(l, 1), chunk_out(l, 1))
        window(True, 1, chunk_out(l, 1), True, 0, use_gu(l, 0), activate, chunk_down(l, 0))
        window(True, 0, chunk_down(l, 0), True, 1, use_gu(l, 1), activate, chunk_down(l, 1))
        return carry

    lax.fori_loop(0, layers, layer, 0)

    def out_copy(h, i, q):
        return pltpu.make_async_copy(
            x.at[in_order[i], q, half_rows(h)],
            out.at[half_rows(h), pl.ds(pl.multiple_of(in_order[i] * wide + q * width, width), width)],
            g_sem.at[(h * chips + i) * CORES + q])

    def store(h):
        def use(i):
            for q in range(CORES):
                out_copy(h, i, q).start()
        return use

    window(True, 1, chunk_down(layers - 1, 1), True, 0, store(0), lambda: None, None, sum_stats=False)
    window(False, 0, None, True, 1, store(1), lambda: None, None, with_stats=False)
    for h in range(HALVES):
        for i in range(chips):
            for q in range(CORES):
                out_copy(h, i, q).wait()


def solution(mesh):
    n_dev = mesh.shape['tp']
    chips = n_dev // CORES

    def local_step(hidden, lengths, k_cache, v_cache, attn_norm, w_qkv, w_out, mlp_norm, w_gate, w_up, w_down):
        layers, rows, seq, _, head_dim = k_cache.shape
        d_model = hidden.shape[1]
        width = d_model // n_dev
        qkv_cols = w_qkv.shape[3]
        group = qkv_cols // head_dim - 2
        ff = w_gate.shape[2]
        half = rows // HALVES
        quart = half // 2
        wide = CORES * width
        heads = group * head_dim
        cosine, sine = rope_tables(lengths, head_dim)
        cfg = (layers, rows, width, head_dim, group, chips, seq)
        vmem = pl.BlockSpec(memory_space=pltpu.VMEM)
        hbm = pl.BlockSpec(memory_space=pl.ANY)
        flops = 2 * layers * rows * d_model * (qkv_cols + heads + 3 * ff)
        dma = pltpu.SemaphoreType.DMA
        return pl.pallas_call(
            functools.partial(kernel, cfg),
            out_shape=jax.ShapeDtypeStruct((rows, d_model), BF16),
            in_specs=[hbm] + [vmem] * 5 + [hbm] * 7,
            out_specs=hbm,
            scratch_shapes=[
                pltpu.VMEM((chips, CORES, rows, width), BF16),
                pltpu.VMEM((half, wide), BF16),
                pltpu.VMEM((rows, 128), F32),
                pltpu.VMEM((rows * group, seq), F32),
                pltpu.VMEM((HALVES, chips, CORES, half, width), BF16),
                pltpu.VMEM((HALVES, 2, CORES, quart, width), BF16),
                pltpu.VMEM((HALVES, 2, quart, width), BF16),
                pltpu.VMEM((HALVES, 2, CORES, quart, width), BF16),
                pltpu.VMEM((HALVES, half, width), BF16),
                pltpu.VMEM((HALVES, 2, quart, width), F32),
                pltpu.VMEM((HALVES, 2, quart, width), F32),
                pltpu.VMEM((HALVES, n_dev, 8, rows), F32),
                pltpu.VMEM((half * group, head_dim), F32),
                pltpu.VMEM((half * group, head_dim), F32),
                pltpu.VMEM((half * group, head_dim), F32),
                pltpu.VMEM((half * group, seq), F32),
                pltpu.VMEM((half, heads), BF16),
                pltpu.VMEM((half, ff), BF16),
                pltpu.VMEM((half, ff), F32),
                pltpu.VMEM((half, ff), F32),
                pltpu.VMEM((chips, wide, ff), BF16),
                pltpu.VMEM((chips, wide, ff), BF16),
                pltpu.VMEM((chips, ff, wide), BF16),
                pltpu.VMEM((rows, seq, head_dim), BF16),
                dma((HALVES, 13)),
                dma((HALVES, chips, CORES, 2)),
                dma((HALVES, n_dev)),
                dma((HALVES, 13)),
                dma((HALVES, 21)),
                dma((13,)),
                dma((16,)),
                dma((16,)),
                dma((chips, CORES)),
            ],
            compiler_params=pltpu.CompilerParams(
                collective_id=0, has_side_effects=True, vmem_limit_bytes=67043328),
            cost_estimate=pl.CostEstimate(flops=flops, bytes_accessed=flops // rows, transcendentals=0),
        )(hidden, lengths.reshape(1, rows), cosine, sine, attn_norm, mlp_norm,
          w_qkv.reshape(layers, d_model, qkv_cols), w_out, w_gate, w_up, w_down,
          k_cache.reshape(layers, rows * seq, head_dim), v_cache.reshape(layers, rows, seq, head_dim))

    cache_spec = P(None, 'dp', None, 'tp', None)
    in_specs = (P('dp', None), P('dp'), cache_spec, cache_spec, P(), P(None, None, 'tp', None),
                P(None, 'tp', None), P(), P(None, None, 'tp'), P(None, None, 'tp'), P(None, 'tp', None))
    return jax.shard_map(local_step, mesh=mesh, in_specs=in_specs, out_specs=P('dp', None), check_vma=False)
```

time: 286 us -> 124 us (0.43)
  Pallas kernels: 0 us -> 120 us
  waiting for transfers between devices: 97.5 us -> 0 us
  matrix products: 83.4 us -> 0 us
  blocking collectives: 62.6 us -> 0 us
  other arithmetic: 15.9 us -> 1.73 us
  between operations: 13.6 us -> 0.02 us
  starting transfers between devices: 7.01 us -> 0 us
    pallas_call x0 -> x1, Pallas kernels: none -> 120 us  [local_step(): pl.pallas_call(functools.partial(kernel, cfg), out_shape=jax.ShapeDtypeSt...]
    dot_general x16 -> x0, matrix products: 83.4 us -> none  [the longest x2 17.8 us: local_step(): jnp.dot(activated, w_down[layer], preferred_element_type=jnp.float32)]
    all_gather x4 -> x0, waiting for transfers between devices: 79.7 us -> none  [reduce_add(): return lax.all_gather(summed, 'tp', axis=1, tiled=True)]
    all_to_all x3 -> x0, blocking collectives: 62.6 us -> none  [reduce_add(): lax.all_to_all(partial.reshape(rows, group_devs, width), 'tp', 1, 1, tile...]
    all_to_all x1 -> x0, waiting for transfers between devices: 17.6 us -> none  [reduce_add(): lax.all_to_all(partial.reshape(rows, group_devs, width), 'tp', 1, 1, tile...]
    reduce_sum x10 -> x0, other arithmetic: 8.05 us -> none  [the longest x4 6.6 us: rms_norm(): scale = lax.rsqrt(jnp.mean(wide * wide, axis=-1, keepdims=True) + NORM_EPS)]
    all_to_all x1 -> x0, starting transfers between devices: 6.15 us -> none  [reduce_add(): lax.all_to_all(partial.reshape(rows, group_devs, width), 'tp', 1, 1, tile...]
    convert_element_type x7 -> x1, other arithmetic: 5.4 us -> 0.66 us  [rope_tables(): angles = lengths.astype(F32)[:, None] * inv_freq[None, :]]
  transfers between devices with their start and end apart: 5 -> 0, of which waited for: 5 -> 0; matrix products, arithmetic and copies ran while one was open for 0% -> 0% of each run, Pallas kernels for 0% -> 0%
where the time goes in v2:
time: 124 us
  Pallas kernels  120 us (97%)
  local copies, waits for them, and re-layouts  2.46 us (2%)
  other arithmetic  1.73 us (1%)
    pallas_call x1, Pallas kernels, local_step(): pl.pallas_call(functools.partial(kernel, cfg), out_shape=jax.ShapeDtypeSt...  120 us

profile of v2, /device:TPU:113, one launch (start us, length us, event | category | flops | bytes accessed | tf_op | source)
XLA Modules:
  0.0 123.9 jit_solution(15974410445900076938)
XLA Ops:
  0.0 0.7 convert_element_type.3
  0.7 0.3 fusion
  1.0 0.7 pad_maximum_fusion
  1.7 119.7 %shard_map.109 = bf16[128,5120]{1,0:T(8,128)(2,1)} custom-call(bf16[128,5120]{1,0:T(8,128)(2,1)} %hid.1, s32[1,128]{1,0:T(1,128)} %bitcast.7, f32[128,128]{1,0:T(8,128)} %get-tuple-element.8.cos_ref, f32[128,128]{1,0:T(8,128)} %get-tuple-element.9.sin_ref, bf16[2,5120]{1,0:T(2,128)(2,1)} %gain_attn.1, bf16[2,5120]{1,0:T(2,128)(2,1)} %gain_mlp.1, ...), custom_call_target="tpu_custom_call" | custom-call | flops 17448304640 | bytes 136314880 | tf_op jit(solution)/shard_map/pallas_call | solution.py:483
  121.5 2.5 %copy.13 = bf16[128,5120]{1,0:T(8,128)(2,1)} copy(bf16[128,5120]{1,0:T(8,128)(2,1)} %shard_map.109) | data formatting | bytes 2621440
  (1 shorter events, 0.0 us)

commit v3 on v1

--- a/solution.py
+++ b/solution.py
@@ -2,6 +2,7 @@
 
 import jax
 import jax.numpy as jnp
+import numpy as np
 from jax import lax
 from jax.experimental import pallas as pl
 from jax.experimental.pallas import tpu as pltpu
@@ -15,21 +16,15 @@
 CORES = 2
 GU_SLOTS = 5
 DN_SLOTS = 2
+SPLIT = 4
 NEG = -1e30
 
 
-def rope_tables(lengths, head_dim):
-    inv_freq = ROPE_BASE ** (-jnp.arange(0, head_dim, 2, dtype=F32) / head_dim)
-    angles = lengths.astype(F32)[:, None] * inv_freq[None, :]
-    cosine, sine = jnp.cos(angles), jnp.sin(angles)
-    return jnp.concatenate([cosine, cosine], 1), jnp.concatenate([-sine, sine], 1)
-
-
-def kernel(cfg, hid, lens, cos_ref, sin_ref, gain_attn, gain_mlp, wqkv, wout, wgate, wup, wdown, kc, vc, out,
-           x, a_buf, rbuf, lrep, part, rel_in, prt_in, dir_in, own_in, f_out, f_in, stat,
+def kernel(cfg, hid, lens, freq, gain_attn, gain_mlp, wqkv, wout, wgate, wup, wdown, kc, vc, out,
+           x, a_buf, rbuf, lrep, part, rel_in, prt_in, dir_in, own_in, f_out, f_in, stat, squares, cos_ref, sin_ref,
            q_s, kn_s, vn_s, s_s, attn, act, g_acc, u_acc,
            b_qkv, b_out, b_k, b_v, b_gu, b_d,
-           rs_sem, ag_sem, st_sem, snd_sem, snd2_sem, w_sem, x_sem):
+           rs_sem, rel_sem, dir_sem, f_sem, ag_sem, st_sem, snd_sem, snd2_sem, w_sem, x_sem):
     layers, rows, width, head_dim, group, chips, seq = cfg
     half = rows // 2
     wide = CORES * width
@@ -96,6 +91,10 @@
     lens_row = jnp.broadcast_to(lens[...].astype(F32), (rows, rows)).T
     for g in range(group):
         lrep[pl.ds(g, rows, stride=group), :] = lens_row
+    angles = lens_row[:, :head_dim] * freq[...]
+    sine = jnp.sin(angles)
+    cos_ref[...] = jnp.cos(angles)
+    sin_ref[...] = jnp.where(lax.broadcasted_iota(jnp.int32, angles.shape, 1) < head_dim // 2, -sine, sine)
 
     for cp in x_loads:
         cp.wait()
@@ -224,100 +223,134 @@
                 ld_d(n + DN_SLOTS).start()
         return chunk
 
-    def reduce_scatter(chunk):
-        sends = []
-
-        def send(src, dst, rsem, where):
-            cp = pltpu.make_async_remote_copy(
-                src_ref=src, dst_ref=dst, send_sem=snd_sem.at[len(sends)], recv_sem=rsem,
-                device_id=where, device_id_type=MESH)
+    step_rows = half // SPLIT
+
+    def rows_of(w, s):
+        return pl.ds(w * half + s * step_rows, step_rows)
+
+    def remote(src, dst, ssem, rsem, where):
+        return pltpu.make_async_remote_copy(
+            src_ref=src, dst_ref=dst, send_sem=ssem, recv_sem=rsem, device_id=where, device_id_type=MESH)
+
+    me = dev(c, e)
+    mate = dev(c, other)
+
+    def arrived(dst, rsem):
+        remote(dst, dst, rsem, rsem, me).wait_recv()
+
+    class Sends:
+        def __init__(self, sems):
+            self.sems, self.all = sems, []
+
+        def __call__(self, src, dst, rsem, where):
+            cp = remote(src, dst, self.sems.at[len(self.all)], rsem, where)
             cp.start()
-            sends.append(cp)
-
-        def arrived(dst, rsem):
-            pltpu.make_async_remote_copy(
-                src_ref=dst, dst_ref=dst, send_sem=snd_sem.at[0], recv_sem=rsem,
-                device_id=dev(c, e), device_id_type=MESH).wait_recv()
+            self.all.append(cp)
+
+        def done(self):
+            for cp in self.all:
+                cp.wait_send()
+
+    toward = (right, left)
+
+    def reduce_scatter(chunk, finished):
+        send = Sends(snd_sem)
+
+        def piece(s):
+            return pl.ds(s * step_rows, step_rows)
+
+        def send_direct(s):
+            for q in range(CORES):
+                send(part.at[1, q, rows_of(1, s)], dir_in.at[1, e, piece(s)], dir_sem.at[1, e, s], dev(right, q))
+                send(part.at[2, q, rows_of(0, s)], dir_in.at[0, e, piece(s)], dir_sem.at[0, e, s], dev(left, q))
 
         chunk(0)
-        for q in range(CORES):
-            send(part.at[0, q, first], rel_in.at[0, e], rs_sem.at[e], dev(right, q))
-            send(part.at[0, q, second], rel_in.at[1, e], rs_sem.at[2 + e], dev(left, q))
+        for s in range(SPLIT):
+            for q in range(CORES):
+                for w in range(2):
+                    send(part.at[0, q, rows_of(w, s)], rel_in.at[w, e, piece(s)], rel_sem.at[w, e, s],
+                         dev(toward[w], q))
         chunk(1)
-        send(part.at[1, other, first], prt_in.at[0], rs_sem.at[4], dev(c, other))
-        for q in range(CORES):
-            send(part.at[1, q, second], dir_in.at[1, e], rs_sem.at[8 + e], dev(right, q))
+        send(part.at[1, other, first], prt_in.at[0], rs_sem.at[0], mate)
         chunk(2)
-        send(part.at[2, other, second], prt_in.at[1], rs_sem.at[5], dev(c, other))
-        for q in range(CORES):
-            send(part.at[2, q, first], dir_in.at[0, e], rs_sem.at[6 + e], dev(left, q))
+        send(part.at[2, other, second], prt_in.at[1], rs_sem.at[1], mate)
+        send_direct(0)
         chunk(3)
-        send(part.at[3, other], own_in, rs_sem.at[12], dev(c, other))
-        for way in range(2):
-            where = (first, second)[way]
-            for q in range(CORES):
-                arrived(rel_in.at[way, q], rs_sem.at[2 * way + q])
-            arrived(prt_in.at[way], rs_sem.at[4 + way])
-            f_out[way] = (rel_in[way, 0].astype(F32) + rel_in[way, 1].astype(F32)
-                          + (prt_in[way].astype(F32) + part[1 + way, e, where].astype(F32)))
-            send(f_out.at[way], f_in.at[way], rs_sem.at[10 + way], dev((right, left)[way], e))
-        arrived(own_in, rs_sem.at[12])
-        squares = []
-        for way in range(2):
-            where = (first, second)[way]
-            for q in range(CORES):
-                arrived(dir_in.at[way, q], rs_sem.at[6 + 2 * way + q])
-            arrived(f_in.at[way], rs_sem.at[10 + way])
-            h = ((part[3, e, where].astype(F32) + own_in[where].astype(F32))
-                 + (dir_in[way, 0].astype(F32) + dir_in[way, 1].astype(F32)) + f_in[way])
-            h = (x[c, e, where].astype(F32) + h).astype(BF16)
-            x[c, e, where] = h
-            h = h.astype(F32)
-            sq = h * h
-            tot = sq[:, :128]
-            for j in range(1, width // 128):
-                tot = tot + sq[:, j * 128:(j + 1) * 128]
-            squares.append(tot)
-        for cp in sends:
-            cp.wait_send()
-        return jnp.concatenate(squares, axis=0)
-
-    def all_gather(squares, consume):
-        sends = []
-
-        def send(src, dst, rsem, where):
-            cp = pltpu.make_async_remote_copy(
-                src_ref=src, dst_ref=dst, send_sem=snd2_sem.at[len(sends)], recv_sem=rsem,
-                device_id=where, device_id_type=MESH)
-            cp.start()
-            sends.append(cp)
-
-        def arrived(dst, rsem):
-            pltpu.make_async_remote_copy(
-                src_ref=dst, dst_ref=dst, send_sem=snd2_sem.at[0], recv_sem=rsem,
-                device_id=dev(c, e), device_id_type=MESH).wait_recv()
-
-        ranges = (first, second)
-
-        def push(chip, core, way, where):
-            ref = x.at[chip, core, ranges[way]]
-            send(ref, ref, ag_sem.at[chip, core, way], where)
-
-        def have(chip, core, way):
-            arrived(x.at[chip, core, ranges[way]], ag_sem.at[chip, core, way])
-
-        if squares is not None:
-            row = jnp.sum(squares.T, axis=0, keepdims=True)
-            stat[tp] = jnp.broadcast_to(row, (8, rows))
-            for step in range(1, n_dev):
-                send(stat.at[tp], stat.at[tp], st_sem.at[tp], {'tp': lax.rem(tp + step, n_dev)})
-        push(c, e, 0, dev(right, e))
-        push(c, e, 1, dev(left, e))
-        push(c, e, 1, dev(right, e))
-        push(c, e, 0, dev(left, e))
-        push(c, e, 0, dev(c, other))
-        push(c, e, 1, dev(c, other))
-        if squares is not None:
+        send(part.at[3, other], own_in, rs_sem.at[2], mate)
+        for w in range(2):
+            arrived(prt_in.at[w], rs_sem.at[w])
+        for s in range(SPLIT):
+            at = slice(s * step_rows, (s + 1) * step_rows)
+            for w in range(2):
+                for q in range(CORES):
+                    arrived(rel_in.at[w, q, piece(s)], rel_sem.at[w, q, s])
+                f_out[w, at] = (rel_in[w, 0, at].astype(F32) + rel_in[w, 1, at].astype(F32)
+                                + (prt_in[w, at].astype(F32) + part[1 + w, e, rows_of(w, s)].astype(F32)))
+                send(f_out.at[w, piece(s)], f_in.at[w, piece(s)], f_sem.at[w, s], dev(toward[w], e))
+            if s + 1 < SPLIT:
+                send_direct(s + 1)
+        arrived(own_in, rs_sem.at[2])
+        for s in range(SPLIT):
+            at = slice(s * step_rows, (s + 1) * step_rows)
+            for w in range(2):
+                where = rows_of(w, s)
+                for q in range(CORES):
+                    arrived(dir_in.at[w, q, piece(s)], dir_sem.at[w, q, s])
+                arrived(f_in.at[w, piece(s)], f_sem.at[w, s])
+                v = ((part[3, e, where].astype(F32) + own_in[where].astype(F32))
+                     + (dir_in[w, 0, at].astype(F32) + dir_in[w, 1, at].astype(F32)) + f_in[w, at])
+                v = (x[c, e, where].astype(F32) + v).astype(BF16)
+                x[c, e, where] = v
+                v = v.astype(F32)
+                sq = v * v
+                tot = sq[:, :128]
+                for j in range(1, width // 128):
+                    tot = tot + sq[:, j * 128:(j + 1) * 128]
+                squares[where, :] = tot
+            finished(s)
+        send.done()
+
+    def reduce(chunk, consume, with_stats=True):
+        send = Sends(snd2_sem)
+
+        def push(chip, core, w, s, where):
+            ref = x.at[chip, core, rows_of(w, s)]
+            send(ref, ref, ag_sem.at[chip, core, w, s], where)
+
+        def have(chip, core, w, s):
+            arrived(x.at[chip, core, rows_of(w, s)], ag_sem.at[chip, core, w, s])
+
+        def have_all(chip, core):
+            for s in range(SPLIT):
+                for w in range(2):
+                    have(chip, core, w, s)
+
+        def finished(s):
+            if with_stats and s == SPLIT - 1:
+                row = jnp.sum(squares[...].T, axis=0, keepdims=True)
+                stat[tp] = jnp.broadcast_to(row, (8, rows))
+                for step in range(1, n_dev):
+                    send(stat.at[tp], stat.at[tp], st_sem.at[tp], {'tp': lax.rem(tp + step, n_dev)})
+            push(c, e, 0, s, dev(right, e))
+            push(c, e, 1, s, dev(left, e))
+            push(c, e, 1, s, dev(right, e))
+            push(c, e, 0, s, dev(left, e))
+            push(c, e, 0, s, mate)
+            push(c, e, 1, s, mate)
+
+        reduce_scatter(chunk, finished)
+        for s in range(SPLIT):
+            have(left, e, 0, s)
+            push(left, e, 0, s, dev(right, e))
+            push(left, e, 0, s, mate)
+            have(right, e, 1, s)
+            push(right, e, 1, s, dev(left, e))
+            push(right, e, 1, s, mate)
+            have(left, e, 1, s)
+            push(left, e, 1, s, mate)
+            have(right, e, 0, s)
+            push(right, e, 0, s, mate)
+        if with_stats:
             for step in range(1, n_dev):
                 src = lax.rem(tp + step, n_dev)
                 arrived(stat.at[src], st_sem.at[src])
@@ -325,34 +358,19 @@
             for j in range(1, n_dev):
                 row = row + stat[j, 0:1]
             rbuf[...] = jnp.broadcast_to(lax.rsqrt(row / d_model + NORM_EPS), (rows, rows)).T
-        have(c, other, 0)
-        have(c, other, 1)
+        have_all(c, other)
         consume(0)
-        have(left, e, 0)
-        push(left, e, 0, dev(right, e))
-        push(left, e, 0, dev(c, other))
-        have(right, e, 1)
-        push(right, e, 1, dev(left, e))
-        push(right, e, 1, dev(c, other))
-        have(left, e, 1)
-        push(left, e, 1, dev(c, other))
-        have(right, e, 0)
-        push(right, e, 0, dev(c, other))
-        have(left, other, 0)
-        have(left, other, 1)
+        have_all(left, other)
         consume(1)
-        have(far, e, 0)
-        push(far, e, 0, dev(c, other))
-        have(far, e, 1)
-        push(far, e, 1, dev(c, other))
-        have(right, other, 0)
-        have(right, other, 1)
+        for s in range(SPLIT):
+            for w in range(2):
+                have(far, e, w, s)
+                push(far, e, w, s, mate)
+        have_all(right, other)
         consume(2)
-        have(far, other, 0)
-        have(far, other, 1)
+        have_all(far, other)
         consume(3)
-        for cp in sends:
-            cp.wait_send()
+        send.done()
 
     for i in range(chips):
         use_qkv(0)(i)
@@ -363,14 +381,12 @@
         if l == 0:
             for n in range(DN_SLOTS):
                 ld_d(n).start()
-        squares = reduce_scatter(chunk_out(l))
-        all_gather(squares, use_gu(l))
+        reduce(chunk_out(l), use_gu(l))
         gate = g_acc[...].astype(BF16).astype(F32)
         up = u_acc[...].astype(BF16).astype(F32)
         act[...] = (gate * jax.nn.sigmoid(gate) * up).astype(BF16)
-        squares = reduce_scatter(chunk_down(l))
         if l + 1 < layers:
-            all_gather(squares, use_qkv(l + 1))
+            reduce(chunk_down(l), use_qkv(l + 1))
     stores = []
 
     def store(i):
@@ -382,9 +398,37 @@
             cp.start()
             stores.append(cp)
 
-    all_gather(None, store)
+    reduce(chunk_down(layers - 1), store, with_stats=False)
     for cp in stores:
         cp.wait()
+
+
+def emit_kernel(src, dst, buf, in_sem, out_sem):
+    n = in_sem.shape[0]
+    rows = src.shape[0] // n
+
+    def copy_in(i):
+        return pltpu.make_async_copy(src.at[pl.ds(i * rows, rows)], buf.at[pl.ds(i * rows, rows)], in_sem.at[i])
+
+    def copy_out(i):
+        return pltpu.make_async_copy(buf.at[pl.ds(i * rows, rows)], dst.at[pl.ds(i * rows, rows)], out_sem.at[i])
+
+    for i in range(n):
+        copy_in(i).start()
+    for i in range(n):
+        copy_in(i).wait()
+        copy_out(i).start()
+    for i in range(n):
+        copy_out(i).wait()
+
+
+def emit(value):
+    hbm = pl.BlockSpec(memory_space=pl.ANY)
+    return pl.pallas_call(
+        emit_kernel, out_shape=jax.ShapeDtypeStruct(value.shape, value.dtype), in_specs=[hbm], out_specs=hbm,
+        scratch_shapes=[pltpu.VMEM(value.shape, value.dtype), pltpu.SemaphoreType.DMA((4,)),
+                        pltpu.SemaphoreType.DMA((4,))],
+        cost_estimate=pl.CostEstimate(flops=0, bytes_accessed=4 * value.size, transcendentals=0))(value)
 
 
 def solution(mesh):
@@ -401,15 +445,16 @@
         half = rows // 2
         wide = CORES * width
         heads = group * head_dim
-        cosine, sine = rope_tables(lengths, head_dim)
+        inv_freq = (ROPE_BASE ** (-np.arange(0, head_dim, 2, dtype=np.float32) / head_dim)).astype(np.float32)
+        freq = jnp.asarray(np.concatenate([inv_freq, inv_freq])[None, :])
         cfg = (layers, rows, width, head_dim, group, chips, seq)
         vmem = pl.BlockSpec(memory_space=pltpu.VMEM)
         hbm = pl.BlockSpec(memory_space=pl.ANY)
         flops = 2 * layers * rows * d_model * (qkv_cols + heads + 3 * ff)
-        return pl.pallas_call(
+        return emit(pl.pallas_call(
             functools.partial(kernel, cfg),
             out_shape=jax.ShapeDtypeStruct((rows, d_model), BF16),
-            in_specs=[hbm] + [vmem] * 5 + [hbm] * 7,
+            in_specs=[hbm] + [vmem] * 4 + [hbm] * 7,
             out_specs=hbm,
             scratch_shapes=[
                 pltpu.VMEM((chips, CORES, rows, width), BF16),
@@ -424,6 +469,9 @@
                 pltpu.VMEM((2, half, width), F32),
                 pltpu.VMEM((2, half, width), F32),
                 pltpu.VMEM((n_dev, 8, rows), F32),
+                pltpu.VMEM((rows, 128), F32),
+                pltpu.VMEM((rows, head_dim), F32),
+                pltpu.VMEM((rows, head_dim), F32),
                 pltpu.VMEM((rows * group, head_dim), F32),
                 pltpu.VMEM((rows * group, head_dim), F32),
                 pltpu.VMEM((rows * group, head_dim), F32),
@@ -438,20 +486,23 @@
                 pltpu.VMEM((rows, seq, head_dim), BF16),
                 pltpu.VMEM((GU_SLOTS, wide, ff), BF16),
                 pltpu.VMEM((DN_SLOTS, ff, wide), BF16),
-                pltpu.SemaphoreType.DMA((13,)),
-                pltpu.SemaphoreType.DMA((chips, CORES, 2)),
+                pltpu.SemaphoreType.DMA((3,)),
+                pltpu.SemaphoreType.DMA((2, CORES, SPLIT)),
+                pltpu.SemaphoreType.DMA((2, CORES, SPLIT)),
+                pltpu.SemaphoreType.DMA((2, SPLIT)),
+                pltpu.SemaphoreType.DMA((chips, CORES, 2, SPLIT)),
                 pltpu.SemaphoreType.DMA((n_dev,)),
-                pltpu.SemaphoreType.DMA((16,)),
-                pltpu.SemaphoreType.DMA((24,)),
+                pltpu.SemaphoreType.DMA((3 + 10 * SPLIT,)),
+                pltpu.SemaphoreType.DMA((n_dev - 1 + 14 * SPLIT,)),
                 pltpu.SemaphoreType.DMA((10 + GU_SLOTS + DN_SLOTS,)),
                 pltpu.SemaphoreType.DMA((chips, CORES)),
             ],
             compiler_params=pltpu.CompilerParams(
                 collective_id=0, has_side_effects=True, vmem_limit_bytes=67043328),
             cost_estimate=pl.CostEstimate(flops=flops, bytes_accessed=flops // rows, transcendentals=0),
-        )(hidden, lengths.reshape(1, rows), cosine, sine, attn_norm, mlp_norm,
+        )(hidden, lengths.reshape(1, rows), freq, attn_norm, mlp_norm,
           w_qkv.reshape(layers, d_model, qkv_cols), w_out, w_gate, w_up, w_down,
-          k_cache.reshape(layers, rows, seq, head_dim), v_cache.reshape(layers, rows, seq, head_dim))
+          k_cache.reshape(layers, rows, seq, head_dim), v_cache.reshape(layers, rows, seq, head_dim)))
 
     cache_spec = P(None, 'dp', None, 'tp', None)
     in_specs = (P('dp', None), P('dp'), cache_spec, cache_spec, P(), P(None, None, 'tp', None),

time: 129 us -> 126 us (0.977)
  local copies, waits for them, and re-layouts: 2.46 us -> 0 us
  other arithmetic: 1.73 us -> 0 us
    unnamed x1 -> x0, local copies, waits for them, and re-layouts: 2.46 us -> none
    pallas_call x0 -> x1, Pallas kernels: none -> 2.09 us  [emit(): pl.pallas_call(emit_kernel, out_shape=jax.ShapeDtypeStruct(value.shape, v...]
where the time goes in v3:
time: 126 us; the launch traced here: 125 us
  Pallas kernels  125 us (99%)
    pallas_call x1, Pallas kernels, local_step(): pl.pallas_call(functools.partial(kernel, cfg), out_shape=jax.ShapeDtypeSt...  123 us

profile of v3, /device:TPU:113, one launch (start us, length us, event | category | flops | bytes accessed | tf_op | source)
XLA Modules:
  0.0 125.4 jit_solution(14445175514940614349)
XLA Ops:
  0.0 123.1 %shard_map.118.src = bf16[128,5120]{1,0:T(8,128)(2,1)} custom-call(bf16[128,5120]{1,0:T(8,128)(2,1)} %hid.1, s32[1,128]{1,0:T(1,128)} %bitcast.7, f32[1,128]{1,0:T(1,128)} %constant.2.clone.freq, bf16[2,5120]{1,0:T(2,128)(2,1)} %gain_attn.1, bf16[2,5120]{1,0:T(2,128)(2,1)} %gain_mlp.1, bf16[2,5120,768]{2,1,0:T(8,128)(2,1)} %bitcast.4, ...), custom_call_target="tpu_custom_call" | custom-call | flops 17448304640 | bytes 136314880 | tf_op jit(solution)/shard_map/pallas_call | solution.py:454
  123.1 2.1 %shard_map.119 = bf16[128,5120]{1,0:T(8,128)(2,1)} custom-call(bf16[128,5120]{1,0:T(8,128)(2,1)} %shard_map.118.src), custom_call_target="tpu_custom_call" | custom-call | bytes 2621440 | tf_op jit(solution)/shard_map/pallas_call | solution.py:427

commit v4 on v3

--- a/solution.py
+++ b/solution.py
@@ -14,8 +14,7 @@
 BF16 = jnp.bfloat16
 MESH = pl.DeviceIdType.MESH
 CORES = 2
-GU_SLOTS = 5
-DN_SLOTS = 2
+GU_SLOTS = 7
 SPLIT = 4
 NEG = -1e30
 
@@ -23,12 +22,13 @@
 def kernel(cfg, hid, lens, freq, gain_attn, gain_mlp, wqkv, wout, wgate, wup, wdown, kc, vc, out,
            x, a_buf, rbuf, lrep, part, rel_in, prt_in, dir_in, own_in, f_out, f_in, stat, squares, cos_ref, sin_ref,
            q_s, kn_s, vn_s, s_s, attn, act, g_acc, u_acc,
-           b_qkv, b_out, b_k, b_v, b_gu, b_d,
-           rs_sem, rel_sem, dir_sem, f_sem, ag_sem, st_sem, snd_sem, snd2_sem, w_sem, x_sem):
+           b_v, b_gu, b_d,
+           rs_sem, rel_sem, dir_sem, f_sem, ag_sem, st_sem, snd_sem, snd2_sem, w_sem, k_sem, g_sem, x_sem):
     layers, rows, width, head_dim, group, chips, seq = cfg
     half = rows // 2
     wide = CORES * width
     qkv_cols = (group + 2) * head_dim
+    heads = group * head_dim
     d_model = chips * wide
     tp = lax.axis_index('tp')
     e = lax.rem(tp, CORES)
@@ -49,26 +49,41 @@
     in_order = (c, left, right, far)
     out_order = (far, right, left, c)
 
+    def qkv_at(i):
+        return b_d.at[i, 0:wide, 0:qkv_cols]
+
+    def out_at(i):
+        return b_d.at[i, wide:wide + heads, :]
+
+    per_block = wide // seq
+    lane_blocks = (wide - qkv_cols) // head_dim
+    n_blocks = -(-rows // per_block)
+    full_blocks = rows // per_block
+
+    def keys_at(j, first_row, n):
+        lane = pl.multiple_of(qkv_cols + (j % lane_blocks) * head_dim, head_dim)
+        return b_d.at[j // lane_blocks, pl.ds(first_row, n), pl.ds(lane, head_dim)]
+
     def ld_qkv(l, i):
-        return pltpu.make_async_copy(wqkv.at[l, cols(in_order[i]), :], b_qkv.at[i], w_sem.at[i])
+        return pltpu.make_async_copy(wqkv.at[l, cols(in_order[i]), :], qkv_at(i), w_sem.at[i])
 
     def ld_out(l, i):
-        return pltpu.make_async_copy(wout.at[l, :, cols(out_order[i])], b_out.at[i], w_sem.at[4 + i])
-
-    def ld_k(l):
-        return pltpu.make_async_copy(kc.at[l], b_k, w_sem.at[8])
+        return pltpu.make_async_copy(wout.at[l, :, cols(out_order[i])], out_at(i), w_sem.at[4 + i])
+
+    def ld_k(l, j):
+        n = min(per_block, rows - j * per_block) * seq
+        return pltpu.make_async_copy(kc.at[l, pl.ds(j * wide, n), :], keys_at(j, 0, n), k_sem.at[j])
 
     def ld_v(l):
-        return pltpu.make_async_copy(vc.at[l], b_v, w_sem.at[9])
+        return pltpu.make_async_copy(vc.at[l], b_v, w_sem.at[8])
 
     def ld_gu(m):
         l, i, s = m // (2 * chips), m // 2 % chips, m % GU_SLOTS
         src = wup if m % 2 else wgate
-        return pltpu.make_async_copy(src.at[l, cols(in_order[i]), :], b_gu.at[s], w_sem.at[10 + s])
-
-    def ld_d(n):
-        l, i, s = n // chips, n % chips, n % DN_SLOTS
-        return pltpu.make_async_copy(wdown.at[l, :, cols(out_order[i])], b_d.at[s], w_sem.at[10 + GU_SLOTS + s])
+        return pltpu.make_async_copy(src.at[l, cols(in_order[i]), :], b_gu.at[s], g_sem.at[s])
+
+    def ld_d(l, i):
+        return pltpu.make_async_copy(wdown.at[l, :, cols(out_order[i])], b_d.at[i], w_sem.at[9 + i])
 
     x_loads = [pltpu.make_async_copy(
         hid.at[:, pl.ds(k * wide + h * width, width)], x.at[k, h], x_sem.at[k, h])
@@ -77,7 +92,8 @@
         cp.start()
     for i in range(chips):
         ld_qkv(0, i).start()
-    ld_k(0).start()
+    for j in range(n_blocks):
+        ld_k(0, j).start()
     ld_v(0).start()
     for i in range(chips):
         ld_out(0, i).start()
@@ -119,13 +135,11 @@
         def consume(i):
             normed(in_order[i], gain_attn, l)
             ld_qkv(l, i).wait()
-            prod = jnp.dot(a_buf[...], b_qkv[i], preferred_element_type=F32)
+            prod = jnp.dot(a_buf[...], qkv_at(i)[...], preferred_element_type=F32)
             if i == 0:
                 g_acc[:, :qkv_cols] = prod
             else:
                 g_acc[:, :qkv_cols] += prod
-            if l + 1 < layers:
-                ld_qkv(l + 1, i).start()
         return consume
 
     def use_gu(l):
@@ -162,19 +176,24 @@
         scale = head_dim ** -0.5
         pair = 2 * group
         upper = lax.broadcasted_iota(jnp.int32, (pair, head_dim), 0) < group
-        ld_k(l).wait()
-
-        def scores(i, carry):
-            at = pl.ds(pl.multiple_of(i * pair, pair), pair)
-            q = q_s[at, :].astype(BF16)
-            keys = b_k[pl.ds(i * 2, 2)].reshape(2 * seq, head_dim)
-            s = lax.dot_general(q, keys, (((1,), (1,)), ((), ())), preferred_element_type=F32)
+        for j in range(n_blocks):
+            ld_k(l, j).wait()
+
+        def score(j, p):
+            at = pl.ds(pl.multiple_of((j * (per_block // 2) + p) * pair, pair), pair)
+            keys = keys_at(j, p * 2 * seq, 2 * seq)[...]
+            s = lax.dot_general(q_s[at, :].astype(BF16), keys, (((1,), (1,)), ((), ())),
+                                preferred_element_type=F32)
             s_s[at, :] = jnp.where(upper, s[:, :seq], s[:, seq:])
+
+        def scores(j, carry):
+            for p in range(per_block // 2):
+                score(j, p)
             return carry
 
-        lax.fori_loop(0, rows // 2, scores, 0, unroll=8)
-        if l + 1 < layers:
-            ld_k(l + 1).start()
+        lax.fori_loop(0, full_blocks, scores, 0)
+        for p in range((rows - full_blocks * per_block) // 2):
+            score(full_blocks, p)
         pos = lax.broadcasted_iota(jnp.int32, (rows * group, seq), 1).astype(F32)
         s = jnp.where(pos < lrep[...], s_s[...] * scale, NEG)
         own = jnp.sum(q_s[...] * kn_s[...], axis=1, keepdims=True) * scale
@@ -205,22 +224,26 @@
     def chunk_out(l):
         def chunk(i):
             ld_out(l, i).wait()
-            prod = jnp.dot(attn[...], b_out[i], preferred_element_type=F32)
+            prod = jnp.dot(attn[...], out_at(i)[...], preferred_element_type=F32)
+            part[i, 0] = prod[:, :width].astype(BF16)
+            part[i, 1] = prod[:, width:].astype(BF16)
+            ld_d(l, i).start()
+        return chunk
+
+    def chunk_down(l):
+        def chunk(i):
+            ld_d(l, i).wait()
+            prod = jnp.dot(act[...], b_d[i], preferred_element_type=F32)
             part[i, 0] = prod[:, :width].astype(BF16)
             part[i, 1] = prod[:, width:].astype(BF16)
             if l + 1 < layers:
-                ld_out(l + 1, i).start()
-        return chunk
-
-    def chunk_down(l):
-        def chunk(i):
-            n = l * chips + i
-            ld_d(n).wait()
-            prod = jnp.dot(act[...], b_d[n % DN_SLOTS], preferred_element_type=F32)
-            part[i, 0] = prod[:, :width].astype(BF16)
-            part[i, 1] = prod[:, width:].astype(BF16)
-            if n + DN_SLOTS < layers * chips:
-                ld_d(n + DN_SLOTS).start()
+                ld_qkv(l + 1, i).start()
+                for j in range(n_blocks):
+                    if j // lane_blocks == i:
+                        ld_k(l + 1, j).start()
+                if i == chips - 1:
+                    for k in range(chips):
+                        ld_out(l + 1, k).start()
         return chunk
 
     step_rows = half // SPLIT
@@ -378,9 +401,6 @@
         ld_gu(m).start()
     for l in range(layers):
         attention(l)
-        if l == 0:
-            for n in range(DN_SLOTS):
-                ld_d(n).start()
         reduce(chunk_out(l), use_gu(l))
         gate = g_acc[...].astype(BF16).astype(F32)
         up = u_acc[...].astype(BF16).astype(F32)
@@ -480,12 +500,9 @@
                 pltpu.VMEM((rows, ff), BF16),
                 pltpu.VMEM((rows, ff), F32),
                 pltpu.VMEM((rows, ff), F32),
-                pltpu.VMEM((chips, wide, qkv_cols), BF16),
-                pltpu.VMEM((chips, heads, wide), BF16),
-                pltpu.VMEM((rows, seq, head_dim), BF16),
                 pltpu.VMEM((rows, seq, head_dim), BF16),
                 pltpu.VMEM((GU_SLOTS, wide, ff), BF16),
-                pltpu.VMEM((DN_SLOTS, ff, wide), BF16),
+                pltpu.VMEM((chips, ff, wide), BF16),
                 pltpu.SemaphoreType.DMA((3,)),
                 pltpu.SemaphoreType.DMA((2, CORES, SPLIT)),
                 pltpu.SemaphoreType.DMA((2, CORES, SPLIT)),
@@ -494,7 +511,9 @@
                 pltpu.SemaphoreType.DMA((n_dev,)),
                 pltpu.SemaphoreType.DMA((3 + 10 * SPLIT,)),
                 pltpu.SemaphoreType.DMA((n_dev - 1 + 14 * SPLIT,)),
-                pltpu.SemaphoreType.DMA((10 + GU_SLOTS + DN_SLOTS,)),
+                pltpu.SemaphoreType.DMA((13,)),
+                pltpu.SemaphoreType.DMA((16,)),
+                pltpu.SemaphoreType.DMA((GU_SLOTS,)),
                 pltpu.SemaphoreType.DMA((chips, CORES)),
             ],
             compiler_params=pltpu.CompilerParams(
@@ -502,7 +521,7 @@
             cost_estimate=pl.CostEstimate(flops=flops, bytes_accessed=flops // rows, transcendentals=0),
         )(hidden, lengths.reshape(1, rows), freq, attn_norm, mlp_norm,
           w_qkv.reshape(layers, d_model, qkv_cols), w_out, w_gate, w_up, w_down,
-          k_cache.reshape(layers, rows, seq, head_dim), v_cache.reshape(layers, rows, seq, head_dim)))
+          k_cache.reshape(layers, rows * seq, head_dim), v_cache.reshape(layers, rows, seq, head_dim)))
 
     cache_spec = P(None, 'dp', None, 'tp', None)
     in_specs = (P('dp', None), P('dp'), cache_spec, cache_spec, P(), P(None, None, 'tp', None),

time: 126 us -> 122 us (0.968)
  Pallas kernels: 125 us -> 122 us
    pallas_call x1, Pallas kernels: 123 us -> 119 us  [local_step(): pl.pallas_call(functools.partial(kernel, cfg), out_shape=jax.ShapeDtypeSt...]
where the time goes in v4:
time: 122 us
  Pallas kernels  122 us (100%)
    pallas_call x1, Pallas kernels, local_step(): pl.pallas_call(functools.partial(kernel, cfg), out_shape=jax.ShapeDtypeSt...  119 us

profile of v4, /device:TPU:113, one launch (start us, length us, event | category | flops | bytes accessed | tf_op | source)
XLA Modules:
  0.0 121.8 jit_solution(4507279830951434390)
XLA Ops:
  0.0 119.5 %shard_map.118.src = bf16[128,5120]{1,0:T(8,128)(2,1)} custom-call(bf16[128,5120]{1,0:T(8,128)(2,1)} %hid.1, s32[1,128]{1,0:T(1,128)} %bitcast.7, f32[1,128]{1,0:T(1,128)} %constant.2.clone.freq, bf16[2,5120]{1,0:T(2,128)(2,1)} %gain_attn.1, bf16[2,5120]{1,0:T(2,128)(2,1)} %gain_mlp.1, bf16[2,5120,768]{2,1,0:T(8,128)(2,1)} %bitcast.4, ...), custom_call_target="tpu_custom_call" | custom-call | flops 17448304640 | bytes 136314880 | tf_op jit(solution)/shard_map/pallas_call | solution.py:474
  119.5 2.1 %shard_map.119 = bf16[128,5120]{1,0:T(8,128)(2,1)} custom-call(bf16[128,5120]{1,0:T(8,128)(2,1)} %shard_map.118.src), custom_call_target="tpu_custom_call" | custom-call | bytes 2621440 | tf_op jit(solution)/shard_map/pallas_call | solution.py:447

commit v5 on v4

--- a/solution.py
+++ b/solution.py
@@ -16,6 +16,7 @@
 CORES = 2
 GU_SLOTS = 7
 SPLIT = 4
+V_PARTS = 8
 NEG = -1e30
 
 
@@ -23,7 +24,7 @@
            x, a_buf, rbuf, lrep, part, rel_in, prt_in, dir_in, own_in, f_out, f_in, stat, squares, cos_ref, sin_ref,
            q_s, kn_s, vn_s, s_s, attn, act, g_acc, u_acc,
            b_v, b_gu, b_d,
-           rs_sem, rel_sem, dir_sem, f_sem, ag_sem, st_sem, snd_sem, snd2_sem, w_sem, k_sem, g_sem, x_sem):
+           rs_sem, rel_sem, dir_sem, f_sem, ag_sem, mate_sem, st_sem, snd_sem, snd2_sem, w_sem, k_sem, v_sem, g_sem, x_sem):
     layers, rows, width, head_dim, group, chips, seq = cfg
     half = rows // 2
     wide = CORES * width
@@ -71,11 +72,14 @@
         return pltpu.make_async_copy(wout.at[l, :, cols(out_order[i])], out_at(i), w_sem.at[4 + i])
 
     def ld_k(l, j):
-        n = min(per_block, rows - j * per_block) * seq
+        n = (per_block if not isinstance(j, int) or j < full_blocks else rows - j * per_block) * seq
         return pltpu.make_async_copy(kc.at[l, pl.ds(j * wide, n), :], keys_at(j, 0, n), k_sem.at[j])
 
-    def ld_v(l):
-        return pltpu.make_async_copy(vc.at[l], b_v, w_sem.at[8])
+    v_rows = rows // V_PARTS
+
+    def ld_v(l, i):
+        at = pl.ds(i * v_rows, v_rows)
+        return pltpu.make_async_copy(vc.at[l, at], b_v.at[at], v_sem.at[i])
 
     def ld_gu(m):
         l, i, s = m // (2 * chips), m // 2 % chips, m % GU_SLOTS
@@ -94,7 +98,8 @@
         ld_qkv(0, i).start()
     for j in range(n_blocks):
         ld_k(0, j).start()
-    ld_v(0).start()
+    for i in range(V_PARTS):
+        ld_v(0, i).start()
     for i in range(chips):
         ld_out(0, i).start()
 
@@ -123,19 +128,26 @@
     scale0 = lax.rsqrt(jnp.sum(total, axis=1, keepdims=True) / d_model + NORM_EPS)
     rbuf[...] = jnp.broadcast_to(scale0, (rows, 128))
 
-    def normed(chip, gain_ref, l):
+    def normed(chip, gain_ref, l, q):
         r = jnp.concatenate([rbuf[...]] * (width // 128), axis=1)
-        gain = gain_ref[l:l + 1, cols(chip)].astype(F32)
-        for h in range(CORES):
-            piece = x[chip, h].astype(F32)
-            a_buf[:, h * width:(h + 1) * width] = (
-                piece * r * gain[:, h * width:(h + 1) * width]).astype(BF16)
+        at = pl.ds(pl.multiple_of(chip * wide + q * width, width), width)
+        gain = gain_ref[l:l + 1, at].astype(F32)
+        return (x[chip, q].astype(F32) * r * gain).astype(BF16)
+
+    def take(i, q, gain_ref, l):
+        if q is None:
+            for k in range(CORES):
+                a_buf[:, k * width:(k + 1) * width] = normed(in_order[i], gain_ref, l, k)
+            return a_buf, pl.ds(0, wide)
+        a_buf[:, 0:width] = normed(in_order[i], gain_ref, l, q)
+        return a_buf.at[:, 0:width], pl.ds(pl.multiple_of(q * width, width), width)
 
     def use_qkv(l):
-        def consume(i):
-            normed(in_order[i], gain_attn, l)
-            ld_qkv(l, i).wait()
-            prod = jnp.dot(a_buf[...], qkv_at(i)[...], preferred_element_type=F32)
+        def consume(i, q=None):
+            a, at = take(i, q, gain_attn, l)
+            if q is not other:
+                ld_qkv(l, i).wait()
+            prod = jnp.dot(a[...], qkv_at(i).at[at, :][...], preferred_element_type=F32)
             if i == 0:
                 g_acc[:, :qkv_cols] = prod
             else:
@@ -143,17 +155,18 @@
         return consume
 
     def use_gu(l):
-        def consume(i):
-            normed(in_order[i], gain_mlp, l)
+        def consume(i, q=None):
+            a, at = take(i, q, gain_mlp, l)
             for j, acc in enumerate((g_acc, u_acc)):
                 m = 2 * (l * chips + i) + j
-                ld_gu(m).wait()
-                prod = jnp.dot(a_buf[...], b_gu[m % GU_SLOTS], preferred_element_type=F32)
+                if q is not other:
+                    ld_gu(m).wait()
+                prod = jnp.dot(a[...], b_gu[m % GU_SLOTS, at, :], preferred_element_type=F32)
                 if i == 0:
                     acc[...] = prod
                 else:
                     acc[...] += prod
-                if m + GU_SLOTS < layers * chips * 2:
+                if q is not e and m + GU_SLOTS < layers * chips * 2:
                     ld_gu(m + GU_SLOTS).start()
         return consume
 
@@ -176,9 +189,6 @@
         scale = head_dim ** -0.5
         pair = 2 * group
         upper = lax.broadcasted_iota(jnp.int32, (pair, head_dim), 0) < group
-        for j in range(n_blocks):
-            ld_k(l, j).wait()
-
         def score(j, p):
             at = pl.ds(pl.multiple_of((j * (per_block // 2) + p) * pair, pair), pair)
             keys = keys_at(j, p * 2 * seq, 2 * seq)[...]
@@ -187,11 +197,14 @@
             s_s[at, :] = jnp.where(upper, s[:, :seq], s[:, seq:])
 
         def scores(j, carry):
+            ld_k(l, j).wait()
             for p in range(per_block // 2):
                 score(j, p)
             return carry
 
         lax.fori_loop(0, full_blocks, scores, 0)
+        if full_blocks < n_blocks:
+            ld_k(l, full_blocks).wait()
         for p in range((rows - full_blocks * per_block) // 2):
             score(full_blocks, p)
         pos = lax.broadcasted_iota(jnp.int32, (rows * group, seq), 1).astype(F32)
@@ -204,20 +217,23 @@
         s_s[...] = w
         q_s[...] = w_own * vn_s[...]
         kn_s[...] = jnp.broadcast_to(denom, kn_s.shape)
-        ld_v(l).wait()
 
         def mix(i, carry):
-            at = pl.ds(pl.multiple_of(i * pair, pair), pair)
-            w = s_s[at, :].astype(BF16)
-            vals = jnp.concatenate([b_v[i * 2], b_v[i * 2 + 1]], axis=1)
-            o = jnp.dot(w, vals, preferred_element_type=F32)
-            o = jnp.where(upper, o[:, :head_dim], o[:, head_dim:])
-            s_s[at, :] = (o + q_s[at, :]) / kn_s[at, :]
+            ld_v(l, i).wait()
+            for p in range(v_rows // 2):
+                n = i * (v_rows // 2) + p
+                at = pl.ds(pl.multiple_of(n * pair, pair), pair)
+                w = s_s[at, :].astype(BF16)
+                vals = jnp.concatenate([b_v[n * 2], b_v[n * 2 + 1]], axis=1)
+                o = jnp.dot(w, vals, preferred_element_type=F32)
+                o = jnp.where(upper, o[:, :head_dim], o[:, head_dim:])
+                s_s[at, :] = (o + q_s[at, :]) / kn_s[at, :]
             return carry
 
-        lax.fori_loop(0, rows // 2, mix, 0, unroll=8)
+        lax.fori_loop(0, V_PARTS, mix, 0)
         if l + 1 < layers:
-            ld_v(l + 1).start()
+            for i in range(V_PARTS):
+                ld_v(l + 1, i).start()
         for g in range(group):
             attn[:, g * head_dim:(g + 1) * head_dim] = s_s[pl.ds(g, rows, stride=group), :].astype(BF16)
 
@@ -343,36 +359,38 @@
         def have(chip, core, w, s):
             arrived(x.at[chip, core, rows_of(w, s)], ag_sem.at[chip, core, w, s])
 
-        def have_all(chip, core):
-            for s in range(SPLIT):
-                for w in range(2):
-                    have(chip, core, w, s)
+        def share(chip):
+            ref = x.at[chip, e]
+            send(ref, ref, mate_sem.at[chip], mate)
+
+        def shared(chip):
+            arrived(x.at[chip, other], mate_sem.at[chip])
 
         def finished(s):
+            push(c, e, 0, s, dev(right, e))
+            push(c, e, 1, s, dev(left, e))
             if with_stats and s == SPLIT - 1:
                 row = jnp.sum(squares[...].T, axis=0, keepdims=True)
                 stat[tp] = jnp.broadcast_to(row, (8, rows))
                 for step in range(1, n_dev):
                     send(stat.at[tp], stat.at[tp], st_sem.at[tp], {'tp': lax.rem(tp + step, n_dev)})
-            push(c, e, 0, s, dev(right, e))
-            push(c, e, 1, s, dev(left, e))
             push(c, e, 1, s, dev(right, e))
             push(c, e, 0, s, dev(left, e))
-            push(c, e, 0, s, mate)
-            push(c, e, 1, s, mate)
+            if s == SPLIT - 1:
+                share(c)
 
         reduce_scatter(chunk, finished)
         for s in range(SPLIT):
             have(left, e, 0, s)
             push(left, e, 0, s, dev(right, e))
-            push(left, e, 0, s, mate)
             have(right, e, 1, s)
             push(right, e, 1, s, dev(left, e))
-            push(right, e, 1, s, mate)
+        for s in range(SPLIT):
             have(left, e, 1, s)
-            push(left, e, 1, s, mate)
+        share(left)
+        for s in range(SPLIT):
             have(right, e, 0, s)
-            push(right, e, 0, s, mate)
+        share(right)
         if with_stats:
             for step in range(1, n_dev):
                 src = lax.rem(tp + step, n_dev)
@@ -381,18 +399,19 @@
             for j in range(1, n_dev):
                 row = row + stat[j, 0:1]
             rbuf[...] = jnp.broadcast_to(lax.rsqrt(row / d_model + NORM_EPS), (rows, rows)).T
-        have_all(c, other)
+        shared(c)
         consume(0)
-        have_all(left, other)
+        shared(left)
         consume(1)
         for s in range(SPLIT):
             for w in range(2):
                 have(far, e, w, s)
-                push(far, e, w, s, mate)
-        have_all(right, other)
+        share(far)
+        shared(right)
         consume(2)
-        have_all(far, other)
-        consume(3)
+        consume(3, e)
+        shared(far)
+        consume(3, other)
         send.done()
 
     for i in range(chips):
@@ -409,7 +428,9 @@
             reduce(chunk_down(l), use_qkv(l + 1))
     stores = []
 
-    def store(i):
+    def store(i, q=None):
+        if q is not None and q is e:
+            return
         for h in range(CORES):
             cp = pltpu.make_async_copy(
                 x.at[in_order[i], h],
@@ -446,8 +467,8 @@
     hbm = pl.BlockSpec(memory_space=pl.ANY)
     return pl.pallas_call(
         emit_kernel, out_shape=jax.ShapeDtypeStruct(value.shape, value.dtype), in_specs=[hbm], out_specs=hbm,
-        scratch_shapes=[pltpu.VMEM(value.shape, value.dtype), pltpu.SemaphoreType.DMA((4,)),
-                        pltpu.SemaphoreType.DMA((4,))],
+        scratch_shapes=[pltpu.VMEM(value.shape, value.dtype), pltpu.SemaphoreType.DMA((8,)),
+                        pltpu.SemaphoreType.DMA((8,))],
         cost_estimate=pl.CostEstimate(flops=0, bytes_accessed=4 * value.size, transcendentals=0))(value)
 
 
@@ -508,11 +529,13 @@
                 pltpu.SemaphoreType.DMA((2, CORES, SPLIT)),
                 pltpu.SemaphoreType.DMA((2, SPLIT)),
                 pltpu.SemaphoreType.DMA((chips, CORES, 2, SPLIT)),
+                pltpu.SemaphoreType.DMA((chips,)),
                 pltpu.SemaphoreType.DMA((n_dev,)),
                 pltpu.SemaphoreType.DMA((3 + 10 * SPLIT,)),
-                pltpu.SemaphoreType.DMA((n_dev - 1 + 14 * SPLIT,)),
+                pltpu.SemaphoreType.DMA((n_dev + 3 + 6 * SPLIT,)),
                 pltpu.SemaphoreType.DMA((13,)),
                 pltpu.SemaphoreType.DMA((16,)),
+                pltpu.SemaphoreType.DMA((V_PARTS,)),
                 pltpu.SemaphoreType.DMA((GU_SLOTS,)),
                 pltpu.SemaphoreType.DMA((chips, CORES)),
             ],

time: 122 us -> 121 us (level)
  no operation moved by 1% of the time
where the time goes in v5:
time: 121 us
  Pallas kernels  121 us (100%)
    pallas_call x1, Pallas kernels, local_step(): pl.pallas_call(functools.partial(kernel, cfg), out_shape=jax.ShapeDtypeSt...  119 us

profile of v5, /device:TPU:113, one launch (start us, length us, event | category | flops | bytes accessed | tf_op | source)
XLA Modules:
  0.0 121.0 jit_solution(2724253173251876435)
XLA Ops:
  0.0 118.6 %shard_map.118.src = bf16[128,5120]{1,0:T(8,128)(2,1)} custom-call(bf16[128,5120]{1,0:T(8,128)(2,1)} %hid.1, s32[1,128]{1,0:T(1,128)} %bitcast.7, f32[1,128]{1,0:T(1,128)} %constant.2.clone.freq, bf16[2,5120]{1,0:T(2,128)(2,1)} %gain_attn.1, bf16[2,5120]{1,0:T(2,128)(2,1)} %gain_mlp.1, bf16[2,5120,768]{2,1,0:T(8,128)(2,1)} %bitcast.4, ...), custom_call_target="tpu_custom_call" | custom-call | flops 17448304640 | bytes 136314880 | tf_op jit(solution)/shard_map/pallas_call | solution.py:495
  118.7 2.2 %shard_map.119 = bf16[128,5120]{1,0:T(8,128)(2,1)} custom-call(bf16[128,5120]{1,0:T(8,128)(2,1)} %shard_map.118.src), custom_call_target="tpu_custom_call" | custom-call | bytes 2621440 | tf_op jit(solution)/shard_map/pallas_call | solution.py:468

commit v6 on v5

--- a/solution.py
+++ b/solution.py
@@ -16,7 +16,7 @@
 CORES = 2
 GU_SLOTS = 7
 SPLIT = 4
-V_PARTS = 8
+V_PARTS = 4
 NEG = -1e30
 
 
@@ -196,13 +196,19 @@
                                 preferred_element_type=F32)
             s_s[at, :] = jnp.where(upper, s[:, :seq], s[:, seq:])
 
-        def scores(j, carry):
+        def scores(n, carry):
+            for k in range(2):
+                ld_k(l, n * 2 + k).wait()
+            for k in range(2):
+                for p in range(per_block // 2):
+                    score(n * 2 + k, p)
+            return carry
+
+        lax.fori_loop(0, full_blocks // 2, scores, 0)
+        for j in range(full_blocks // 2 * 2, full_blocks):
             ld_k(l, j).wait()
             for p in range(per_block // 2):
                 score(j, p)
-            return carry
-
-        lax.fori_loop(0, full_blocks, scores, 0)
         if full_blocks < n_blocks:
             ld_k(l, full_blocks).wait()
         for p in range((rows - full_blocks * per_block) // 2):
@@ -237,21 +243,27 @@
         for g in range(group):
             attn[:, g * head_dim:(g + 1) * head_dim] = s_s[pl.ds(g, rows, stride=group), :].astype(BF16)
 
-    def chunk_out(l):
-        def chunk(i):
-            ld_out(l, i).wait()
-            prod = jnp.dot(attn[...], out_at(i)[...], preferred_element_type=F32)
+    def multiply(a, w, i, sent):
+        if sent is None:
+            prod = jnp.dot(a[...], w[...], preferred_element_type=F32)
             part[i, 0] = prod[:, :width].astype(BF16)
             part[i, 1] = prod[:, width:].astype(BF16)
+            return
+        for q in range(CORES):
+            part[i, q] = jnp.dot(a[...], w[:, q * width:(q + 1) * width], preferred_element_type=F32).astype(BF16)
+            sent(q)
+
+    def chunk_out(l):
+        def chunk(i, sent=None):
+            ld_out(l, i).wait()
+            multiply(attn, out_at(i), i, sent)
             ld_d(l, i).start()
         return chunk
 
     def chunk_down(l):
-        def chunk(i):
+        def chunk(i, sent=None):
             ld_d(l, i).wait()
-            prod = jnp.dot(act[...], b_d[i], preferred_element_type=F32)
-            part[i, 0] = prod[:, :width].astype(BF16)
-            part[i, 1] = prod[:, width:].astype(BF16)
+            multiply(act, b_d.at[i], i, sent)
             if l + 1 < layers:
                 ld_qkv(l + 1, i).start()
                 for j in range(n_blocks):
@@ -303,12 +315,13 @@
                 send(part.at[1, q, rows_of(1, s)], dir_in.at[1, e, piece(s)], dir_sem.at[1, e, s], dev(right, q))
                 send(part.at[2, q, rows_of(0, s)], dir_in.at[0, e, piece(s)], dir_sem.at[0, e, s], dev(left, q))
 
-        chunk(0)
-        for s in range(SPLIT):
-            for q in range(CORES):
+        def send_far(q):
+            for s in range(SPLIT):
                 for w in range(2):
                     send(part.at[0, q, rows_of(w, s)], rel_in.at[w, e, piece(s)], rel_sem.at[w, e, s],
                          dev(toward[w], q))
+
+        chunk(0, send_far)
         chunk(1)
         send(part.at[1, other, first], prt_in.at[0], rs_sem.at[0], mate)
         chunk(2)

time: 121 us -> 116 us (0.959)
  Pallas kernels: 121 us -> 116 us
    pallas_call x1, Pallas kernels: 119 us -> 114 us  [local_step(): pl.pallas_call(functools.partial(kernel, cfg), out_shape=jax.ShapeDtypeSt...]
where the time goes in v6:
time: 116 us
  Pallas kernels  116 us (100%)
    pallas_call x1, Pallas kernels, local_step(): pl.pallas_call(functools.partial(kernel, cfg), out_shape=jax.ShapeDtypeSt...  114 us

profile of v6, /device:TPU:113, one launch (start us, length us, event | category | flops | bytes accessed | tf_op | source)
XLA Modules:
  0.0 115.9 jit_solution(17894431912027770388)
XLA Ops:
  0.0 113.5 %shard_map.118.src = bf16[128,5120]{1,0:T(8,128)(2,1)} custom-call(bf16[128,5120]{1,0:T(8,128)(2,1)} %hid.1, s32[1,128]{1,0:T(1,128)} %bitcast.7, f32[1,128]{1,0:T(1,128)} %constant.2.clone.freq, bf16[2,5120]{1,0:T(2,128)(2,1)} %gain_attn.1, bf16[2,5120]{1,0:T(2,128)(2,1)} %gain_mlp.1, bf16[2,5120,768]{2,1,0:T(8,128)(2,1)} %bitcast.4, ...), custom_call_target="tpu_custom_call" | custom-call | flops 17448304640 | bytes 136314880 | tf_op jit(solution)/shard_map/pallas_call | solution.py:508
  113.5 2.2 %shard_map.119 = bf16[128,5120]{1,0:T(8,128)(2,1)} custom-call(bf16[128,5120]{1,0:T(8,128)(2,1)} %shard_map.118.src), custom_call_target="tpu_custom_call" | custom-call | bytes 2621440 | tf_op jit(solution)/shard_map/pallas_call | solution.py:481

commit v7 on v6

--- a/solution.py
+++ b/solution.py
@@ -16,7 +16,8 @@
 CORES = 2
 GU_SLOTS = 7
 SPLIT = 4
-V_PARTS = 4
+V_PARTS = 2
+TRIP_BLOCKS = 3
 NEG = -1e30
 
 
@@ -197,15 +198,15 @@
             s_s[at, :] = jnp.where(upper, s[:, :seq], s[:, seq:])
 
         def scores(n, carry):
-            for k in range(2):
-                ld_k(l, n * 2 + k).wait()
-            for k in range(2):
+            for k in range(TRIP_BLOCKS):
+                ld_k(l, n * TRIP_BLOCKS + k).wait()
+            for k in range(TRIP_BLOCKS):
                 for p in range(per_block // 2):
-                    score(n * 2 + k, p)
+                    score(n * TRIP_BLOCKS + k, p)
             return carry
 
-        lax.fori_loop(0, full_blocks // 2, scores, 0)
-        for j in range(full_blocks // 2 * 2, full_blocks):
+        lax.fori_loop(0, full_blocks // TRIP_BLOCKS, scores, 0)
+        for j in range(full_blocks // TRIP_BLOCKS * TRIP_BLOCKS, full_blocks):
             ld_k(l, j).wait()
             for p in range(per_block // 2):
                 score(j, p)
@@ -416,12 +417,12 @@
         consume(0)
         shared(left)
         consume(1)
+        shared(right)
+        consume(2)
         for s in range(SPLIT):
             for w in range(2):
                 have(far, e, w, s)
         share(far)
-        shared(right)
-        consume(2)
         consume(3, e)
         shared(far)
         consume(3, other)

time: 116 us -> 116 us (level)
  no operation moved by 1% of the time
where the time goes in v7:
time: 116 us
  Pallas kernels  116 us (100%)
    pallas_call x1, Pallas kernels, local_step(): pl.pallas_call(functools.partial(kernel, cfg), out_shape=jax.ShapeDtypeSt...  113 us

profile of v7, /device:TPU:113, one launch (start us, length us, event | category | flops | bytes accessed | tf_op | source)
XLA Modules:
  0.0 115.7 jit_solution(3529992386939281084)
XLA Ops:
  0.0 113.4 %shard_map.118.src = bf16[128,5120]{1,0:T(8,128)(2,1)} custom-call(bf16[128,5120]{1,0:T(8,128)(2,1)} %hid.1, s32[1,128]{1,0:T(1,128)} %bitcast.7, f32[1,128]{1,0:T(1,128)} %constant.2.clone.freq, bf16[2,5120]{1,0:T(2,128)(2,1)} %gain_attn.1, bf16[2,5120]{1,0:T(2,128)(2,1)} %gain_mlp.1, bf16[2,5120,768]{2,1,0:T(8,128)(2,1)} %bitcast.4, ...), custom_call_target="tpu_custom_call" | custom-call | flops 17448304640 | bytes 136314880 | tf_op jit(solution)/shard_map/pallas_call | solution.py:509
  113.4 2.2 %shard_map.119 = bf16[128,5120]{1,0:T(8,128)(2,1)} custom-call(bf16[128,5120]{1,0:T(8,128)(2,1)} %shard_map.118.src), custom_call_target="tpu_custom_call" | custom-call | bytes 2621440 | tf_op jit(solution)/shard_map/pallas_call | solution.py:482

commit v8 on v7

--- a/solution.py
+++ b/solution.py
@@ -311,8 +311,8 @@
         def piece(s):
             return pl.ds(s * step_rows, step_rows)
 
-        def send_direct(s):
-            for q in range(CORES):
+        def send_direct(q):
+            for s in range(SPLIT):
                 send(part.at[1, q, rows_of(1, s)], dir_in.at[1, e, piece(s)], dir_sem.at[1, e, s], dev(right, q))
                 send(part.at[2, q, rows_of(0, s)], dir_in.at[0, e, piece(s)], dir_sem.at[0, e, s], dev(left, q))
 
@@ -340,8 +340,7 @@
                 f_out[w, at] = (rel_in[w, 0, at].astype(F32) + rel_in[w, 1, at].astype(F32)
                                 + (prt_in[w, at].astype(F32) + part[1 + w, e, rows_of(w, s)].astype(F32)))
                 send(f_out.at[w, piece(s)], f_in.at[w, piece(s)], f_sem.at[w, s], dev(toward[w], e))
-            if s + 1 < SPLIT:
-                send_direct(s + 1)
+        send_direct(1)
         arrived(own_in, rs_sem.at[2])
         for s in range(SPLIT):
             at = slice(s * step_rows, (s + 1) * step_rows)

time: 116 us -> 116 us (level)
  no operation moved by 1% of the time
where the time goes in v8:
time: 116 us
  Pallas kernels  116 us (100%)
    pallas_call x1, Pallas kernels, local_step(): pl.pallas_call(functools.partial(kernel, cfg), out_shape=jax.ShapeDtypeSt...  114 us

profile of v8, /device:TPU:113, one launch (start us, length us, event | category | flops | bytes accessed | tf_op | source)
XLA Modules:
  0.0 116.1 jit_solution(5107836448394928093)
XLA Ops:
  0.0 113.7 %shard_map.118.src = bf16[128,5120]{1,0:T(8,128)(2,1)} custom-call(bf16[128,5120]{1,0:T(8,128)(2,1)} %hid.1, s32[1,128]{1,0:T(1,128)} %bitcast.7, f32[1,128]{1,0:T(1,128)} %constant.2.clone.freq, bf16[2,5120]{1,0:T(2,128)(2,1)} %gain_attn.1, bf16[2,5120]{1,0:T(2,128)(2,1)} %gain_mlp.1, bf16[2,5120,768]{2,1,0:T(8,128)(2,1)} %bitcast.4, ...), custom_call_target="tpu_custom_call" | custom-call | flops 17448304640 | bytes 136314880 | tf_op jit(solution)/shard_map/pallas_call | solution.py:508
  113.7 2.2 %shard_map.119 = bf16[128,5120]{1,0:T(8,128)(2,1)} custom-call(bf16[128,5120]{1,0:T(8,128)(2,1)} %shard_map.118.src), custom_call_target="tpu_custom_call" | custom-call | bytes 2621440 | tf_op jit(solution)/shard_map/pallas_call | solution.py:481
